TPU v7x, 32 devices: a whole 2x2x4 slice. The times are simulated.
32 devices in a mesh: sub: 4 (over y, x), rng: 8 (over z, core).
Axes of the slice: x: 2, y: 2, z: 4, core: 2. Of those that a mesh axis runs over, the one named last changes fastest.
Arguments:
- echoes: float32 [512, 2, 12288], P(('sub', 'rng')), may hold values from -6 to 6
- filter_spectrum: float32 [2, 12288], replicated, may hold values from -3 to 3
- range_shifts: int32 [512], P('sub'), may hold values from -16 to 16
- steering: bfloat16 [4, 2, 384, 128], P('sub'), may hold values from -0.375 to 0.375
- tap_offsets: int32 [4, 2, 384], P('sub'), may hold values from -3 to 3
- tap_weights: float32 [4, 2, 4, 384], P('sub'), may hold values from -2 to 2
- phase_rates: float32 [4, 2, 384], P('sub'), may hold values from -6 to 6
Outputs:
- tiles: float32 [1536, 2, 12288], P('sub', None, 'rng')
All inputs are finite; a program needn't handle non-finite values.
Results may differ from a plain program's by a relative error of at most 0.0076.
Values may be sent and summed in bfloat16 or wider, within the bound.
No kernel may reach another device: no remote copies, remote signals or barrier semaphores. Data moves between devices by JAX's collectives and lax.ppermute only.
A program may use at most 256 MiB of HBM per device.

v0:
```python
import functools
import math

import jax
import jax.numpy as jnp
import numpy as np
from jax import lax
from jax.experimental import pallas as pl
from jax.experimental.layout import Layout, with_layout_constraint
from jax.experimental.pallas import tpu as pltpu
from jax.sharding import PartitionSpec as P


LANES = 128
QUAD = 4
F32 = jnp.float32
BF16 = jnp.bfloat16
MERGE_LIMIT = 16 * 1024 * 1024
REACH = 6
UNIT = 4
LOADS = 11
PASSES = (3, 3, 1, 1)
COMPRESS_LIMIT = 60 * 1024 * 1024


def split_table(table):
    high = table.astype(np.float32).astype(BF16)
    low = (table - high.astype(np.float64)).astype(np.float32).astype(BF16)
    return np.stack([high, low])


def frequency_order(radix):
    sections = math.lcm(radix, LANES) // radix
    place = np.arange(LANES)
    return sections * (place % (LANES // sections)) + place // (LANES // sections)


@functools.lru_cache(None)
def dft_tables(samples):
    radix = samples // LANES
    outer = 2.0 * np.pi * (np.outer(np.arange(radix), np.arange(radix)) % radix) / radix
    inner = 2.0 * np.pi * (np.outer(np.arange(LANES), np.arange(LANES)) % LANES) / LANES
    turn = 2.0 * np.pi * np.outer(np.arange(radix), np.arange(LANES)) / samples
    c, s = np.cos(outer), np.sin(outer)
    first = np.concatenate(
        [np.stack([c, s], -1).reshape(radix, -1), np.stack([-s, c], -1).reshape(radix, -1)]
    )
    last = np.block([[c, -s], [s, c]]) / samples
    order = frequency_order(radix)
    c, s = np.cos(inner)[:, order], np.sin(inner)[:, order]
    forward = np.block([[c, -s], [s, c]])
    backward = np.block([[c.T, s.T], [-s.T, c.T]])
    twiddle = np.stack([np.cos(turn), np.sin(turn)]).astype(np.float32)
    return (
        split_table(first),
        split_table(forward),
        split_table(backward),
        split_table(last),
        twiddle,
    )


def halves(x):
    high = x.astype(BF16)
    return high, (x - high.astype(F32)).astype(BF16)


def dot(a, b):
    return jnp.dot(a, b, preferred_element_type=F32)


def table_dot(table, x, passes=3):
    if passes == 1:
        return dot(table[0], x.astype(BF16))
    high, low = halves(x)
    if passes == 2:
        return dot(table[0], high) + dot(table[0], low)
    return dot(table[0], high) + dot(table[0], low) + dot(table[1], high)


def dot_table(x, table, passes=3):
    if passes == 1:
        return dot(x.astype(BF16), table[0])
    high, low = halves(x)
    if passes == 2:
        return dot(high, table[0]) + dot(low, table[0])
    return dot(high, table[0]) + dot(low, table[0]) + dot(high, table[1])


def encode(early, base, taps_ref, offsets_ref, rates_ref):
    angles = rates_ref.shape[-1]
    empty = jnp.zeros((4, angles), F32)
    left = jnp.concatenate(
        [taps_ref[0, 0], taps_ref[0, 1], offsets_ref[0].astype(F32), rates_ref[0], empty], axis=0
    )
    for piece in range(3):
        high = left.astype(BF16)
        left = left - high.astype(F32)
        for at in range(angles // LANES):
            spot = base + 16 * (piece * (angles // LANES) + at)
            early[spot : spot + 16, :LANES] = high[:, at * LANES : (at + 1) * LANES]


def decode(ref, base, angles):
    pieces = []
    for piece in range(3):
        spots = [base + 16 * (piece * (angles // LANES) + at) for at in range(angles // LANES)]
        pieces.append(
            jnp.concatenate([ref[spot : spot + 16, :LANES] for spot in spots], axis=1).astype(F32)
        )
    return pieces[0] + pieces[1] + pieces[2]


def load_filter(raw_ref, filt_ref):
    radix = filt_ref.shape[1]
    period = math.lcm(radix, LANES)
    sections, rows = period // radix, period // LANES
    count = LANES // sections
    lane = lax.broadcasted_iota(jnp.int32, (count, LANES), 1)
    for part in range(2):
        near = [raw_ref[pl.ds(2 * o + part, count, stride=2 * rows), :] for o in range(rows)]
        stack = []
        for u in range(sections):
            at, skip = divmod(radix * u, LANES)
            cells = near[at]
            if skip:
                cells = pltpu.roll(cells, LANES - skip, 1)
                if skip + radix > LANES:
                    after = pltpu.roll(near[at + 1], LANES - skip, 1)
                    cells = jnp.where(lane < LANES - skip, cells, after)
            stack.append(cells)
        filt_ref[part] = jnp.transpose(jnp.concatenate(stack, axis=0))[:radix]


def compress_kernel(ranks, me_ref, shifts_ref, *refs):
    loads, (near, odd, early) = refs[:LOADS], refs[LOADS : LOADS + 3]
    total, filt_ref, *held = refs[LOADS + 3 : -1]
    done = refs[-1]
    echo_ref, first_ref, twiddle_ref, raw_ref, forward_ref, backward_ref, last_ref = held[:7]
    taps_ref, offsets_ref, rates_ref = held[7:]
    held = [*held, early.at[pl.ds(0, loads[-1].shape[0])]]

    def piece(step):
        cells = pl.ds(step * QUAD, QUAD)
        return pltpu.make_async_copy(
            loads[0].at[cells], echo_ref.at[cells], done.at[LOADS + step]
        )

    copies = [pltpu.make_async_copy(loads[i], held[i], done.at[i]) for i in range(1, LOADS)]
    first, twiddle, raw, forward, backward, last = copies[:6]
    first.start()
    piece(0).start()
    twiddle.start()
    for step in range(1, echo_ref.shape[0] // QUAD):
        piece(step).start()
    for copy in (*copies[6:], raw, forward, backward, last):
        copy.start()
    first.wait()
    pulses, radix = echo_ref.shape[0], echo_ref.shape[1] // 2
    wide = 2 * pulses
    me = me_ref[0]
    lane = lax.broadcasted_iota(jnp.int32, (radix, LANES), 1)
    row = lax.broadcasted_iota(jnp.int32, (radix, LANES), 0)
    sections = []
    for step in range(pulses // QUAD):
        piece(step).wait()
        x = jnp.concatenate([echo_ref[step * QUAD + q] for q in range(QUAD)], axis=1)
        y = table_dot(first_ref, x, PASSES[0])
        if not step:
            twiddle.wait()
        for q in range(QUAD):
            here = slice(q * LANES, (q + 1) * LANES)
            turned = complex_times((y[:radix, here], y[radix:, here]), (twiddle_ref[0], -twiddle_ref[1]))
            sections.append(jnp.concatenate(turned, axis=1))
    for copy in (*copies[6:], raw, forward, backward, last):
        copy.wait()
    load_filter(raw_ref, filt_ref)
    encode(early, loads[-1].shape[0], taps_ref, offsets_ref, rates_ref)
    z = dot_table(jnp.concatenate(sections, axis=0), forward_ref, PASSES[1])
    sections = []
    for q in range(pulses):
        here = slice(q * radix, (q + 1) * radix)
        turned = complex_times((z[here, :LANES], z[here, LANES:]), (filt_ref[0], filt_ref[1]))
        sections.append(jnp.concatenate(turned, axis=1))
    z = dot_table(jnp.concatenate(sections, axis=0), backward_ref, PASSES[2])
    sections = []
    for q in range(pulses):
        here = slice(q * radix, (q + 1) * radix)
        turned = complex_times((z[here, :LANES], z[here, LANES:]), (twiddle_ref[0], twiddle_ref[1]))
        sections.append(jnp.concatenate(turned, axis=0))
    y = table_dot(last_ref, jnp.concatenate(sections, axis=1), PASSES[3])
    for q in range(pulses):
        shift = shifts_ref[me * pulses + q]
        source = lane + shift
        for part in range(2):
            cells = y[part * radix : (part + 1) * radix, q * LANES : (q + 1) * LANES]
            turned = pltpu.roll(cells, lax.rem(LANES - shift, LANES), 1)
            after = jnp.where(row == radix - 1, 0.0, pltpu.roll(turned, radix - 1, 0))
            before = jnp.where(row == 0, 0.0, pltpu.roll(turned, 1, 0))
            moved = jnp.where(source >= LANES, after, jnp.where(source < 0, before, turned))
            total[pl.ds(part * pulses + q, radix, stride=wide), :] = moved

    length = radix // ranks * wide
    for d in range(ranks):
        start = pl.multiple_of(lax.bitwise_xor(me, d) * length, 8)
        target = odd if d % 2 else near
        target[d // 2] = total[pl.ds(start, length), :].astype(BF16)


def compress(echoes, filter_spectrum, range_shifts, steering, tap_offsets, tap_weights, phase_rates, me, ranks):
    pulses, _, samples = echoes.shape
    radix = samples // LANES
    wide = 2 * pulses
    view = echoes.reshape(pulses, 2, radix, LANES).transpose(0, 2, 1, 3)
    view = view.reshape(pulses, 2 * radix, LANES)
    filt = filter_spectrum.reshape(2, radix, LANES).transpose(1, 0, 2).reshape(2 * radix, LANES)
    angles = steering.shape[2]
    steer = steering.reshape(2 * angles, -1)
    first, forward, backward, last, twiddle = [jnp.asarray(t) for t in dft_tables(samples)]
    loads = [view, first, twiddle, filt, forward, backward, last]
    loads += [tap_weights, tap_offsets, phase_rates, steer]
    smem = pl.BlockSpec(memory_space=pltpu.SMEM)
    vmem = pl.BlockSpec(memory_space=pltpu.VMEM)
    away = pl.BlockSpec(memory_space=pltpu.HBM)
    half = ranks // 2
    return pl.pallas_call(
        functools.partial(compress_kernel, ranks),
        out_shape=[
            jax.ShapeDtypeStruct((half, radix // ranks * wide, LANES), BF16) for _ in range(2)
        ]
        + [jax.ShapeDtypeStruct((2 * angles + 48 * angles // LANES, steer.shape[1]), BF16)],
        in_specs=[smem, smem] + [away] * LOADS,
        out_specs=[vmem] * 3,
        scratch_shapes=[pltpu.VMEM((radix * wide, LANES), F32), pltpu.VMEM((2, radix, LANES), F32)]
        + [pltpu.VMEM(x.shape, x.dtype) for x in loads[:-1]]
        + [pltpu.SemaphoreType.DMA((LOADS + pulses // QUAD,))],
        compiler_params=pltpu.CompilerParams(vmem_limit_bytes=COMPRESS_LIMIT),
        cost_estimate=pl.CostEstimate(
            flops=pulses * samples * 4000, bytes_accessed=pulses * samples * 12, transcendentals=0
        ),
        name="compress",
    )(me, range_shifts, *loads)


def pack_kernel(cuts, wide, *refs):
    near, far, *outs = refs
    half = far.shape[0]
    for cut, (low, high) in enumerate(cuts):
        for z in range(half):
            outs[cut * half + z][0] = near[z, low * wide : high * wide]
            outs[cut * half + z][1] = far[z, low * wide : high * wide]


def pack(near, far, cuts, wide):
    half = far.shape[0]
    vmem = pl.BlockSpec(memory_space=pltpu.VMEM)
    flat = pl.pallas_call(
        functools.partial(pack_kernel, cuts, wide),
        out_shape=[
            jax.ShapeDtypeStruct((2, (high - low) * wide, LANES), BF16)
            for low, high in cuts
            for _ in range(half)
        ],
        in_specs=[vmem] * 2,
        out_specs=[vmem] * (len(cuts) * half),
        compiler_params=pltpu.CompilerParams(vmem_limit_bytes=16 * 1024 * 1024),
        cost_estimate=pl.CostEstimate(flops=1 << 20, bytes_accessed=1 << 20, transcendentals=0),
        name="pack",
    )(near, far)
    return [flat[cut * half : (cut + 1) * half] for cut in range(len(cuts))]


def twice(a):
    double = a[1] + a[1]
    return 1.0 - double * a[1], double * a[0]


def complex_times(a, b):
    return a[0] * b[0] - a[1] * b[1], a[0] * b[1] + a[1] * b[0]


def prepare_kernel(groups, ranks, rows, samples, pair, cuts, me_ref, *refs):
    steer = refs[:groups]
    mixes, mats, *turns = refs[groups:]
    places = [(cut, at) for cut, (low, high) in enumerate(cuts) for at in range((high - low) // pair)]
    angles = mats.shape[-1]
    members = steer[0].shape[-1]
    me = me_ref[0]
    share = members // ranks
    column = lax.broadcasted_iota(jnp.int32, (members, 2 * members), 1)
    member = lax.broadcasted_iota(jnp.int32, (members, 2 * members), 0)
    slot = lax.div(column, 2 * share)
    within = lax.rem(column, 2 * share)
    part = lax.div(within, share)
    source = lax.bitwise_xor(slot, me) * share + lax.rem(within, share)
    picks = [
        jnp.where((part == c) & (source == member), 1.0, 0.0).astype(BF16) for c in range(2)
    ]
    below = lax.broadcasted_iota(jnp.int32, (angles, angles), 0)
    across = lax.broadcasted_iota(jnp.int32, (1, angles), 1)
    lane = lax.broadcasted_iota(jnp.int32, (angles, LANES), 1)
    small = lane.astype(F32) * (1.0 / samples)
    tables = [decode(steer[2 * pick], 2 * angles, angles) for pick in range(groups // 2)]
    rates = jnp.concatenate([table[10:12] for table in tables], axis=0)
    begin = rates * ((me * (rows * LANES)).astype(F32) * (1.0 / samples))
    lines = [rates, jnp.cos(begin), jnp.sin(begin)]
    for count in (1, pair):
        phase = rates * (count * LANES / samples)
        lines += [jnp.cos(phase), jnp.sin(phase)]
    lines.append(jnp.zeros((LANES - 7 * groups, angles), F32))
    lines = jnp.transpose(jnp.concatenate(lines, axis=0))

    def spread(kind, n):
        at = kind * groups + n
        return jnp.broadcast_to(lines[:, at : at + 1], (angles, LANES))

    for pick in range(groups // 2):
        offset = 2 * pick
        table = tables[pick]
        for h in range(2):
            moved = table[8 + h : 9 + h, :].astype(jnp.int32)
            total = jnp.zeros((angles, angles), F32)
            for tap in range(4):
                at_row = jnp.clip(across + moved + (tap - 1), 0, angles - 1)
                total = total + jnp.where(below == at_row, table[4 * h + tap : 4 * h + tap + 1, :], 0.0)
            matrix = jnp.transpose(total).astype(BF16)
            mats[2 * pick + h] = matrix
            near = steer[offset ^ h]
            real = dot(matrix, near[:angles, :]).astype(BF16)
            imag = dot(matrix, near[angles : 2 * angles, :]).astype(BF16)
            mixes[2 * pick + h, :angles, :] = (dot(real, picks[0]) - dot(imag, picks[1])).astype(BF16)
            mixes[2 * pick + h, angles:, :] = (dot(imag, picks[0]) + dot(real, picks[1])).astype(BF16)
            n = 2 * pick + h
            now = complex_times((spread(1, n), spread(2, n)), small_turn(spread(0, n) * small))
            first = now
            step = (spread(3, n), spread(4, n))
            for u in range(pair):
                here = slice(u * LANES, (u + 1) * LANES)
                if u:
                    first = complex_times(first, step)
                now = first
                jump = (spread(5, n), spread(6, n))
                for index, (cut, at) in enumerate(places):
                    if index:
                        now = complex_times(now, jump)
                    turns[cut][at, n, 0, :, here], turns[cut][at, n, 1, :, here] = now


def small_turn(x):
    y = x * x
    cosine = 1.0 - y * (0.5 - y * (1.0 / 24.0 - y * (1.0 / 720.0)))
    return cosine, x * (1.0 - y * (1.0 / 6.0 - y * (1.0 / 120.0 - y * (1.0 / 5040.0))))


def prepare(steer, angles, me, groups, ranks, rows, samples, pair, cuts):
    members = steer[0].shape[1]
    smem = pl.BlockSpec(memory_space=pltpu.SMEM)
    vmem = pl.BlockSpec(memory_space=pltpu.VMEM)
    return pl.pallas_call(
        functools.partial(prepare_kernel, groups, ranks, rows, samples, pair, cuts),
        out_shape=[
            jax.ShapeDtypeStruct((groups, 2 * angles, 2 * members), BF16),
            jax.ShapeDtypeStruct((groups, angles, angles), BF16),
        ]
        + [
            jax.ShapeDtypeStruct(((high - low) // pair, groups, 2, angles, pair * LANES), F32)
            for low, high in cuts
        ],
        in_specs=[smem] + [vmem] * len(steer),
        out_specs=[vmem] * (2 + len(cuts)),
        compiler_params=pltpu.CompilerParams(vmem_limit_bytes=32 * 1024 * 1024),
        cost_estimate=pl.CostEstimate(
            flops=groups * angles * members * 40000, bytes_accessed=8 << 20, transcendentals=0
        ),
        name="prepare",
    )(me, *steer)


BAND = 32


def direct(source):
    return source & (source - 1) == 0


def kinds(groups):
    whole = [p for p in range(groups // 2) if direct(2 * p) and direct(2 * p + 1)]
    half = [p for p in range(groups // 2) if direct(2 * p) and not direct(2 * p + 1)]
    return whole, half


def columns(parts, wide, base, pair):
    return jnp.concatenate(
        [
            jnp.concatenate(
                [
                    ref[:, pl.ds(pl.multiple_of((base + u) * wide, 8), wide), :].reshape(-1, LANES)
                    for ref in parts
                ],
                axis=0,
            )
            for u in range(pair)
        ],
        axis=1,
    )


def rotated(mixed, turns, at, n, level, top, angles):
    band = slice(top, top + BAND)
    lower = slice(angles + top, angles + top + BAND)
    now = (turns[at, n, 0, band], turns[at, n, 1, band])
    power = twice(now) if level else now
    for _ in range(level - 1):
        power = complex_times(power, now)
    return complex_times((mixed[n, band], mixed[n, lower]), power)


def add(a, b):
    return a[0] + b[0], a[1] + b[1]


def near_kernel(groups, count, layout, mixes, turns, *refs):
    image, partial, mixed = refs[-3:]
    held = split(refs[:-3], layout)
    whole, half = kinds(groups)
    pair, angles = turns.shape[-1] // LANES, turns.shape[-2]
    wide = held[0][0].shape[1] // (count * pair)

    @pl.loop(0, count)
    def _(step):
        here = step
        cells = {o: columns(parts, wide, step * pair, pair) for o, parts in held.items()}
        ready = [n for n in range(groups) if direct(n)]
        for n in ready:
            mixed[n] = dot(mixes[n], cells[n])
        for pick in range(groups // 2):
            terms = [n for n in (2 * pick, 2 * pick + 1) if n in ready]
            for top in range(0, angles if terms else 0, BAND):
                band = slice(top, top + BAND)
                total = rotated(mixed, turns, here, terms[0], 0, top, angles)
                if len(terms) == 2:
                    total = add(total, rotated(mixed, turns, here, terms[1], 0, top, angles))
                    side = pair * LANES
                    image[step, whole.index(pick), band, :side] = total[0].astype(BF16)
                    image[step, whole.index(pick), band, side:] = total[1].astype(BF16)
                else:
                    spot = half.index(pick)
                    partial[step, spot, 0, band], partial[step, spot, 1, band] = total


def far_kernel(groups, count, layout, unit, mixes, mats, turns, image, partial, *refs):
    out, mixed, images = refs[-3:]
    held = split(refs[: sum(len(parts) for parts in layout.values())], layout)
    levels = groups.bit_length() - 1
    whole, half = kinds(groups)
    pair, angles = turns.shape[-1] // LANES, turns.shape[-2]
    wide = held[groups - 1][0].shape[1] // (count * pair)
    side = pair * LANES
    started = pl.program_id(0) * (unit // pair)
    middle = angles // 2
    window = min(angles, -(-(middle + REACH) // LANES) * LANES)
    if len(out.shape) == 3:
        out = out.reshape(out.shape[0] * out.shape[1], LANES)

    @pl.loop(0, unit // pair)
    def _(step):
        place = started + step
        here = place
        cells = {o: columns(parts, wide, place * pair, pair) for o, parts in held.items()}
        late = [n for n in range(groups) if n in held]
        for n in late:
            mixed[n] = dot(mixes[n], cells[n])
        for pick in range(groups // 2):
            terms = [n for n in (2 * pick, 2 * pick + 1) if n in late]
            if not terms:
                images[pick] = image[place, whole.index(pick)]
                continue
            for top in range(0, angles, BAND):
                band = slice(top, top + BAND)
                total = rotated(mixed, turns, here, terms[0], 0, top, angles)
                if len(terms) == 2:
                    total = add(total, rotated(mixed, turns, here, terms[1], 0, top, angles))
                else:
                    spot = half.index(pick)
                    total = add(total, (partial[place, spot, 0, band], partial[place, spot, 1, band]))
                images[pick, band, :side] = total[0].astype(BF16)
                images[pick, band, side:] = total[1].astype(BF16)
        for level in range(1, levels):
            last = level == levels - 1
            stride = 2 << level
            for offset in range(0, groups, stride):
                for h in range(2):
                    n = offset + h
                    source = images.at[(offset ^ (h << level)) // 2]
                    for low, high, start in ((0, middle, 0), (middle, angles, angles - window)):
                        turned = dot(mats[n, low:high, start : start + window], source[start : start + window])
                        mixed[n, low:high] = turned[:, :side]
                        mixed[n, angles + low : angles + high] = turned[:, side:]
            for offset in range(0, groups, stride):
                for top in range(0, angles, BAND):
                    band = slice(top, top + BAND)
                    re, im = add(
                        rotated(mixed, turns, here, offset, level, top, angles),
                        rotated(mixed, turns, here, offset + 1, level, top, angles),
                    )
                    if not last:
                        images[offset // 2, band, :side] = re.astype(BF16)
                        images[offset // 2, band, side:] = im.astype(BF16)
                        continue
                    for u in range(pair):
                        lanes = slice(u * LANES, (u + 1) * LANES)
                        spot = top * unit * 2 + (step * pair + u) * 2
                        out[pl.ds(spot, BAND, stride=unit * 2), :] = re[:, lanes]
                        out[pl.ds(spot + 1, BAND, stride=unit * 2), :] = im[:, lanes]


def split(refs, layout):
    held, at = {}, 0
    for offset, parts in layout.items():
        held[offset] = refs[at : at + len(parts)]
        at += len(parts)
    return held


def merge_near(held, mixes, turns, low, high):
    groups, pair, angles = mixes.shape[0], turns.shape[-1] // LANES, turns.shape[-2]
    vmem = pl.BlockSpec(memory_space=pltpu.VMEM)
    count = (high - low) // pair
    whole, half = kinds(groups)
    flat = [part for parts in held.values() for part in parts]
    return pl.pallas_call(
        functools.partial(near_kernel, groups, count, held),
        out_shape=[
            jax.ShapeDtypeStruct((count, len(whole), angles, 2 * pair * LANES), BF16),
            jax.ShapeDtypeStruct((count, len(half), 2, angles, pair * LANES), F32),
        ],
        in_specs=[vmem] * (2 + len(flat)),
        out_specs=[vmem] * 2,
        scratch_shapes=[pltpu.VMEM((groups, 2 * angles, pair * LANES), F32)],
        compiler_params=pltpu.CompilerParams(vmem_limit_bytes=MERGE_LIMIT),
        cost_estimate=pl.CostEstimate(
            flops=groups * angles * angles * (high - low) * LANES * 4,
            bytes_accessed=angles * (high - low) * LANES * 8,
            transcendentals=0,
        ),
        name="merge_near",
    )(mixes, turns, *flat)


def merge_far(held, mixes, mats, turns, image, partial, rows, low, high, unit, before):
    groups, pair, angles = mixes.shape[0], turns.shape[-1] // LANES, turns.shape[-2]
    vmem = pl.BlockSpec(memory_space=pltpu.VMEM)
    flat = [part for parts in held.values() for part in parts]
    if unit * 2 % 8:
        shape, block, spot = (angles * rows * 2, LANES), (angles * unit * 2, LANES), lambda i: (0, 0)
    else:
        shape, block = (angles, rows * 2, LANES), (angles, unit * 2, LANES)
        spot = lambda i: (0, low // unit + i, 0)
    operands = [mixes, mats, turns, image, partial, *flat]
    specs = [vmem] * len(operands)
    aliases = {}
    if before is not None:
        aliases[len(operands)] = 0
        operands.append(before)
        specs.append(pl.BlockSpec(memory_space=pltpu.HBM))
    return pl.pallas_call(
        functools.partial(far_kernel, groups, (high - low) // pair, held, unit),
        grid=((high - low) // unit,),
        out_shape=jax.ShapeDtypeStruct(shape, F32),
        in_specs=specs,
        out_specs=pl.BlockSpec(block, spot),
        input_output_aliases=aliases,
        scratch_shapes=[
            pltpu.VMEM((groups, 2 * angles, pair * LANES), F32),
            pltpu.VMEM((groups // 2, angles, 2 * pair * LANES), BF16),
        ],
        compiler_params=pltpu.CompilerParams(vmem_limit_bytes=MERGE_LIMIT),
        cost_estimate=pl.CostEstimate(
            flops=groups * angles * angles * (high - low) * LANES * 4,
            bytes_accessed=angles * (high - low) * LANES * 16,
            transcendentals=0,
        ),
        name="merge_far",
    )(*operands)


def hop(value, axis, offset):
    if not offset:
        return value
    return lax.ppermute(value, axis, [(i, i ^ offset) for i in range(lax.axis_size(axis))])


def neighbours(x, groups):
    return {1 << b: hop(x, "sub", 1 << b) for b in range(groups.bit_length() - 1)}


def others(x, near, groups):
    held = {0: [x]}
    for bit in near:
        held[bit] = [near[bit]]
    slots = x.shape[0]
    for offset in range(groups):
        if offset in held:
            continue
        via = [bit for bit in near if offset & bit]
        edges = [slots * i // len(via) for i in range(len(via) + 1)]
        pieces = []
        for bit, low, high in zip(via, edges[:-1], edges[1:]):
            source = held[offset ^ bit]
            source = source[0] if len(source) == 1 else jnp.concatenate(source, axis=0)
            pieces.append(hop(source[low:high], "sub", bit))
        held[offset] = pieces
    return [held[offset] for offset in range(groups)]


def local(echoes, filter_spectrum, range_shifts, steering, tap_offsets, tap_weights, phase_rates):
    ranks, groups = lax.axis_size("rng"), lax.axis_size("sub")
    pulses, _, samples = echoes.shape
    rows = samples // LANES // ranks
    angles = steering.shape[2]
    me = lax.axis_index("rng").astype(jnp.int32).reshape(1)
    unit = UNIT if rows % UNIT == 0 else rows
    cuts = [(low, low + unit) for low in range(0, rows, unit)]
    batches = [(0, unit)] + ([(unit, rows)] if unit < rows else [])

    near, odd, early = compress(
        echoes, filter_spectrum, range_shifts, steering, tap_offsets, tap_weights, phase_rates,
        me, ranks,
    )
    steers = [hop(early, "sub", e) for e in range(groups)]
    wide = 2 * pulses
    packed = pack(near, hop(odd, "rng", 1), batches, wide)
    batch = []
    for blocks in packed:
        batch.append([hop(block, "rng", 2 * z) for z, block in enumerate(blocks)])
    arrived = [jnp.concatenate(batch[0], axis=0)]
    steers, _ = lax.optimization_barrier((steers, arrived[0]))
    pair = 2 if unit % 2 == 0 else 1
    ready = prepare(steers, angles, me, groups, ranks, rows, samples, pair, cuts)
    if len(batch) > 1:
        batch[1], ready = lax.optimization_barrier((batch[1], ready))
        for at in range(0, batch[1][0].shape[1], unit * wide):
            pieces = [piece[:, at : at + unit * wide] for piece in batch[1]]
            arrived.append(jnp.concatenate(pieces, axis=0))
    mixes, mats, *turns = ready

    nears = []
    for x in arrived:
        nears.append(neighbours(x, groups))
    out = None
    for cut, (low, high) in enumerate(cuts):
        held = others(arrived[cut], nears[cut], groups)
        close = {o: held[o] for o in range(groups) if direct(o)}
        far = {o: held[o] for o in range(groups) if not direct(o)}
        image, partial = merge_near(close, mixes, turns[cut], low, high)
        if cut and cut + 1 < len(cuts):
            nears[cut + 1], image = lax.optimization_barrier((nears[cut + 1], image))
        out = merge_far(far, mixes, mats, turns[cut], image, partial, rows, low, high, unit, out)
        if not cut and len(cuts) > 1:
            nears[1], out = lax.optimization_barrier((nears[1], out))
    out = out.reshape(angles, rows, 2, LANES).transpose(0, 2, 1, 3)
    out = with_layout_constraint(out, Layout(major_to_minor=(0, 2, 1, 3)))
    return out.reshape(angles, 2, rows * LANES)


def solution(mesh):
    placed = (
        P(("sub", "rng"), None, None),
        P(),
        P("sub"),
        P("sub", None, None, None),
        P("sub", None, None),
        P("sub", None, None, None),
        P("sub", None, None),
    )

    return jax.shard_map(
        local, mesh=mesh, in_specs=placed, out_specs=P("sub", None, "rng"), check_vma=False
    )
```

profile of v0, /device:TPU:16, one launch (start us, length us, event | category | flops | bytes accessed | tf_op | source)
XLA Modules:
  0.0 64.6 jit_solution(2735762303404705181)
XLA Ops:
  0.0 7.2 %compress.1 = (bf16[4,384,128]{2,1,0:T(8,128)(2,1)}, bf16[4,384,128]{2,1,0:T(8,128)(2,1)}, bf16[912,128]{1,0:T(8,128)(2,1)}) custom-call(s32[1]{0:T(128)} %bitcast.me_ref, s32[128]{0:T(128)} %shifts_ref.1, f32[16,192,128]{2,1,0:T(8,128)} %bitcast.17, bf16[2,192,192]{2,1,0:T(8,128)(2,1)} %constant.14.clone.refs_1_, f32[2,96,128]{2,1,0:T(8,128)} %constant.18.clone.refs_2_, ...), custom_call_target="tpu_custom_call" | custom-call | flops 786432000 | bytes 2359296 | tf_op jit(solution)/shard_map/compress/pallas_call | solution.py:226
  7.2 0.1 collective-permute-start
  7.3 1.6 %collective-permute-start.4 = (bf16[912,128]{1,0:T(8,128)(2,1)}, bf16[912,128]{1,0:T(8,128)(2,1)S(1)}, u32[]{:S(2)}, u32[]{:S(2)}) collective-permute-start(bf16[912,128]{1,0:T(8,128)(2,1)} %get-tuple-element.57.refs_0_), channel_id=1, source_target_pairs={{0,8},{8,0},{16,24},{24,16},{1,9},{9,1},{17,25},{25,17},{2,10},{10... | collective-permute-start | bytes 700424 | tf_op jit(solution)/shard_map/ppermute | solution.py:590
  8.8 1.5 %collective-permute-start.5 = (bf16[912,128]{1,0:T(8,128)(2,1)}, bf16[912,128]{1,0:T(8,128)(2,1)S(1)}, u32[]{:S(2)}, u32[]{:S(2)}) collective-permute-start(bf16[912,128]{1,0:T(8,128)(2,1)} %get-tuple-element.57.refs_0_), channel_id=1, source_target_pairs={{0,16},{8,24},{16,0},{24,8},{1,17},{9,25},{17,1},{25,9},{2,18},{10... | collective-permute-start | bytes 700424 | tf_op jit(solution)/shard_map/ppermute | solution.py:590
  10.3 0.5 collective-permute-start.6
  10.8 1.0 %copy-done = bf16[4,384,128]{2,1,0:T(8,128)(2,1)S(1)} copy-done((bf16[4,384,128]{2,1,0:T(8,128)(2,1)S(1)}, bf16[4,384,128]{2,1,0:T(8,128)(2,1)}, u32[]{:S(2)}) %copy-start) | copy-done | bytes 393240
  11.8 0.1 pack.1
  11.9 1.6 %collective-permute-start.7 = (bf16[2,128,128]{2,1,0:T(8,128)(2,1)S(1)}, bf16[2,128,128]{2,1,0:T(8,128)(2,1)S(1)}, u32[]{:S(2)}, u32[]{:S(2)}) collective-permute-start(bf16[2,128,128]{2,1,0:T(8,128)(2,1)S(1)} %get-tuple-element.54), channel_id=1, source_target_pairs={{0,2},{1,3},{2,0},{3,1},{4,6},{5,7},{6,4},{7,5},{8,10},{9,11},{10,... | collective-permute-start | bytes 196616 | tf_op jit(solution)/shard_map/ppermute | solution.py:590
  13.5 0.3 collective-permute-start.8
  13.9 2.4 %collective-permute-done.7 = bf16[2,128,128]{2,1,0:T(8,128)(2,1)S(1)} collective-permute-done((bf16[2,128,128]{2,1,0:T(8,128)(2,1)S(1)}, bf16[2,128,128]{2,1,0:T(8,128)(2,1)S(1)}, u32[]{:S(2)}, u32[]{:S(2)}) %collective-permute-start.7) | collective-permute-done | bytes 65568 | tf_op jit(solution)/shard_map/ppermute | solution.py:590
  16.2 0.4 collective-permute-start.9
  16.7 2.1 %collective-permute-done.8 = bf16[2,128,128]{2,1,0:T(8,128)(2,1)S(1)} collective-permute-done((bf16[2,128,128]{2,1,0:T(8,128)(2,1)S(1)}, bf16[2,128,128]{2,1,0:T(8,128)(2,1)S(1)}, u32[]{:S(2)}, u32[]{:S(2)}) %collective-permute-start.8) | collective-permute-done | bytes 65568 | tf_op jit(solution)/shard_map/ppermute | solution.py:590
  18.8 0.6 collective-permute-start.1
  19.4 1.5 %collective-permute-done.9 = bf16[2,128,128]{2,1,0:T(8,128)(2,1)S(1)} collective-permute-done((bf16[2,128,128]{2,1,0:T(8,128)(2,1)S(1)}, bf16[2,128,128]{2,1,0:T(8,128)(2,1)S(1)}, u32[]{:S(2)}, u32[]{:S(2)}) %collective-permute-start.9) | collective-permute-done | bytes 65568 | tf_op jit(solution)/shard_map/ppermute | solution.py:590
  20.8 2.6 %collective-permute-start.2 = (bf16[2,256,128]{2,1,0:T(8,128)(2,1)S(1)}, bf16[2,256,128]{2,1,0:T(8,128)(2,1)S(1)}, u32[]{:S(2)}, u32[]{:S(2)}) collective-permute-start(bf16[2,256,128]{2,1,0:T(8,128)(2,1)S(1)} %get-tuple-element.50), channel_id=1, source_target_pairs={{0,4},{1,5},{2,6},{3,7},{4,0},{5,1},{6,2},{7,3},{8,12},{9,13},{10,... | collective-permute-start | bytes 393224 | tf_op jit(solution)/shard_map/ppermute | solution.py:590
  23.5 2.4 %collective-permute-start.3 = (bf16[2,256,128]{2,1,0:T(8,128)(2,1)S(1)}, bf16[2,256,128]{2,1,0:T(8,128)(2,1)S(1)}, u32[]{:S(2)}, u32[]{:S(2)}) collective-permute-start(bf16[2,256,128]{2,1,0:T(8,128)(2,1)S(1)} %get-tuple-element.51), channel_id=1, source_target_pairs={{0,6},{1,7},{2,4},{3,5},{4,2},{5,3},{6,0},{7,1},{8,14},{9,15},{10,... | collective-permute-start | bytes 393224 | tf_op jit(solution)/shard_map/ppermute | solution.py:590
  25.9 0.0 collective-permute-done.5.refs_2_
  25.9 1.5 %collective-permute-start.14 = (bf16[8,128,128]{2,1,0:T(8,128)(2,1)S(1)}, bf16[8,128,128]{2,1,0:T(8,128)(2,1)S(1)}, u32[]{:S(2)}, u32[]{:S(2)}) collective-permute-start(bf16[8,128,128]{2,1,0:T(8,128)(2,1)S(1)} %constant_dynamic-update-slice_fusion.refs_0_), channel_id=1, source_target_pairs={{0,8},{8,0},{16,24},{24,16},{1,9},{9,1},{17,25},{25,17},{2,10},{10... | collective-permute-start | bytes 786440 | tf_op jit(solution)/shard_map/ppermute | solution.py:590
  27.4 1.5 %collective-permute-start.15 = (bf16[8,128,128]{2,1,0:T(8,128)(2,1)S(1)}, bf16[8,128,128]{2,1,0:T(8,128)(2,1)S(1)}, u32[]{:S(2)}, u32[]{:S(2)}) collective-permute-start(bf16[8,128,128]{2,1,0:T(8,128)(2,1)S(1)} %constant_dynamic-update-slice_fusion.refs_0_), channel_id=1, source_target_pairs={{0,16},{8,24},{16,0},{24,8},{1,17},{9,25},{17,1},{25,9},{2,18},{10... | collective-permute-start | bytes 786440 | tf_op jit(solution)/shard_map/ppermute | solution.py:590
  28.9 0.9 %copy-done.1 = bf16[912,128]{1,0:T(8,128)(2,1)S(1)} copy-done((bf16[912,128]{1,0:T(8,128)(2,1)S(1)}, bf16[912,128]{1,0:T(8,128)(2,1)}, u32[]{:S(2)}) %copy-start.1) | copy-done | bytes 233496
  29.8 5.0 %prepare.1 = (bf16[4,768,256]{2,1,0:T(8,128)(2,1)S(1)}, bf16[4,384,384]{2,1,0:T(8,128)(2,1)S(1)}, f32[2,4,2,384,256]{4,3,2,1,0:T(8,128)S(1)}, f32[2,4,2,384,256]...) custom-call(s32[1]{0:T(128)} %bitcast.me_ref, bf16[912,128]{1,0:T(8,128)(2,1)S(1)} %copy-done.1, ...), custom_call_target="tpu_custom_call" | custom-call | flops 7864320000 | bytes 8388608 | tf_op jit(solution)/shard_map/prepare/pallas_call | solution.py:359
  34.9 0.0 collective-permute-done.1
  34.9 0.0 collective-permute-done.3
  35.0 1.0 %collective-permute-start.16 = (bf16[4,128,128]{2,1,0:T(8,128)(2,1)S(1)}, bf16[4,128,128]{2,1,0:T(8,128)(2,1)S(1)}, u32[]{:S(2)}, u32[]{:S(2)}) collective-permute-start(bf16[4,128,128]{2,1,0:T(8,128)(2,1)S(1)} %slice.56), channel_id=1, source_target_pairs={{0,8},{8,0},{16,24},{24,16},{1,9},{9,1},{17,25},{25,17},{2,10},{10... | collective-permute-start | bytes 393224 | tf_op jit(solution)/shard_map/ppermute | solution.py:590
  36.1 1.1 %collective-permute-start.12 = (bf16[8,128,128]{2,1,0:T(8,128)(2,1)S(1)}, bf16[8,128,128]{2,1,0:T(8,128)(2,1)S(1)}, u32[]{:S(2)}, u32[]{:S(2)}) collective-permute-start(bf16[8,128,128]{2,1,0:T(8,128)(2,1)S(1)} %pad_maximum_fusion.1.refs_0_), channel_id=1, source_target_pairs={{0,8},{8,0},{16,24},{24,16},{1,9},{9,1},{17,25},{25,17},{2,10},{10... | collective-permute-start | bytes 786440 | tf_op jit(solution)/shard_map/ppermute | solution.py:590
  37.2 1.0 %collective-permute-start.13 = (bf16[8,128,128]{2,1,0:T(8,128)(2,1)S(1)}, bf16[8,128,128]{2,1,0:T(8,128)(2,1)S(1)}, u32[]{:S(2)}, u32[]{:S(2)}) collective-permute-start(bf16[8,128,128]{2,1,0:T(8,128)(2,1)S(1)} %pad_maximum_fusion.1.refs_0_), channel_id=1, source_target_pairs={{0,16},{8,24},{16,0},{24,8},{1,17},{9,25},{17,1},{25,9},{2,18},{10... | collective-permute-start | bytes 786440 | tf_op jit(solution)/shard_map/ppermute | solution.py:590
  38.2 0.0 collective-permute-done.14.refs_1_
  38.2 1.1 %collective-permute-start.17 = (bf16[4,128,128]{2,1,0:T(8,128)(2,1)S(1)}, bf16[4,128,128]{2,1,0:T(8,128)(2,1)S(1)}, u32[]{:S(2)}, u32[]{:S(2)}) collective-permute-start(bf16[4,128,128]{2,1,0:T(8,128)(2,1)S(1)} %slice.57), channel_id=1, source_target_pairs={{0,16},{8,24},{16,0},{24,8},{1,17},{9,25},{17,1},{25,9},{2,18},{10... | collective-permute-start | bytes 393224 | tf_op jit(solution)/shard_map/ppermute | solution.py:590
  39.3 1.0 %collective-permute-start.10 = (bf16[8,128,128]{2,1,0:T(8,128)(2,1)S(1)}, bf16[8,128,128]{2,1,0:T(8,128)(2,1)S(1)}, u32[]{:S(2)}, u32[]{:S(2)}) collective-permute-start(bf16[8,128,128]{2,1,0:T(8,128)(2,1)S(1)} %pad_maximum_fusion.refs_0_), channel_id=1, source_target_pairs={{0,8},{8,0},{16,24},{24,16},{1,9},{9,1},{17,25},{25,17},{2,10},{10... | collective-permute-start | bytes 786440 | tf_op jit(solution)/shard_map/ppermute | solution.py:590
  40.4 1.1 %collective-permute-done.16.refs_0_ = bf16[4,128,128]{2,1,0:T(8,128)(2,1)S(1)} collective-permute-done((bf16[4,128,128]{2,1,0:T(8,128)(2,1)S(1)}, bf16[4,128,128]{2,1,0:T(8,128)(2,1)S(1)}, u32[]{:S(2)}, u32[]{:S(2)}) %collective-permute-start.16) | collective-permute-done | bytes 131104 | tf_op jit(solution)/shard_map/ppermute | solution.py:590
  41.4 1.0 %collective-permute-start.11 = (bf16[8,128,128]{2,1,0:T(8,128)(2,1)S(1)}, bf16[8,128,128]{2,1,0:T(8,128)(2,1)S(1)}, u32[]{:S(2)}, u32[]{:S(2)}) collective-permute-start(bf16[8,128,128]{2,1,0:T(8,128)(2,1)S(1)} %pad_maximum_fusion.refs_0_), channel_id=1, source_target_pairs={{0,16},{8,24},{16,0},{24,8},{1,17},{9,25},{17,1},{25,9},{2,18},{10... | collective-permute-start | bytes 786440 | tf_op jit(solution)/shard_map/ppermute | solution.py:590
  42.4 1.4 %merge_near.3 = (bf16[2,1,384,512]{3,2,1,0:T(8,128)(2,1)S(1)}, f32[2,1,2,384,256]{4,3,2,1,0:T(8,128)S(1)}) custom-call(bf16[4,768,256]{2,1,0:T(8,128)(2,1)S(1)} %get-tuple-element.66.mixes, f32[2,4,2,384,256]{4,3,2,1,0:T(8,128)S(1)} %get-tuple-element.74.turns, bf16[8,128,128]{2,1,0:T(8,128)(2,1)S(1)} %constant_dynamic-update-slice_fusion.refs_0_, ...), custom_call_target="tpu_custom_call" | custom-call | flops 1207959552 | bytes 1572864 | tf_op jit(solution)/shard_map/merge_near/pallas_call | solution.py:531
  43.9 5.1 %collective-permute-done.17.refs_1_ = bf16[4,128,128]{2,1,0:T(8,128)(2,1)S(1)} collective-permute-done((bf16[4,128,128]{2,1,0:T(8,128)(2,1)S(1)}, bf16[4,128,128]{2,1,0:T(8,128)(2,1)S(1)}, u32[]{:S(2)}, u32[]{:S(2)}) %collective-permute-start.17) | collective-permute-done | bytes 131104 | tf_op jit(solution)/shard_map/ppermute | solution.py:590
  48.9 2.8 %merge_far.3.refs_2_ = f32[384,24,128]{2,1,0:T(8,128)} custom-call(bf16[4,768,256]{2,1,0:T(8,128)(2,1)S(1)} %get-tuple-element.66.mixes, bf16[4,384,384]{2,1,0:T(8,128)(2,1)S(1)} %get-tuple-element.67.mats, f32[2,4,2,384,256]{4,3,2,1,0:T(8,128)S(1)} %get-tuple-element.74.turns, bf16[2,1,384,512]{3,2,1,0:T(8,128)(2,1)S(1)} %get-tuple-element.75.image, ...), custom_call_target="tpu_custom_call" | custom-call | flops 1207959552 | bytes 3145728 | tf_op jit(solution)/shard_map/merge_far/pallas_call | solution.py:566
  51.7 0.0 collective-permute-done.12.refs_1_
  51.7 0.0 collective-permute-done.13.refs_2_
  51.7 1.3 %collective-permute-start.20 = (bf16[4,128,128]{2,1,0:T(8,128)(2,1)S(1)}, bf16[4,128,128]{2,1,0:T(8,128)(2,1)S(1)}, u32[]{:S(2)}, u32[]{:S(2)}) collective-permute-start(bf16[4,128,128]{2,1,0:T(8,128)(2,1)S(1)} %slice.54), channel_id=1, source_target_pairs={{0,8},{8,0},{16,24},{24,16},{1,9},{9,1},{17,25},{25,17},{2,10},{10... | collective-permute-start | bytes 393224 | tf_op jit(solution)/shard_map/ppermute | solution.py:590
  53.0 1.6 %collective-permute-start.21 = (bf16[4,128,128]{2,1,0:T(8,128)(2,1)S(1)}, bf16[4,128,128]{2,1,0:T(8,128)(2,1)S(1)}, u32[]{:S(2)}, u32[]{:S(2)}) collective-permute-start(bf16[4,128,128]{2,1,0:T(8,128)(2,1)S(1)} %slice.55), channel_id=1, source_target_pairs={{0,16},{8,24},{16,0},{24,8},{1,17},{9,25},{17,1},{25,9},{2,18},{10... | collective-permute-start | bytes 393224 | tf_op jit(solution)/shard_map/ppermute | solution.py:590
  54.6 1.4 %merge_near.4 = (bf16[2,1,384,512]{3,2,1,0:T(8,128)(2,1)S(1)}, f32[2,1,2,384,256]{4,3,2,1,0:T(8,128)S(1)}) custom-call(bf16[4,768,256]{2,1,0:T(8,128)(2,1)S(1)} %get-tuple-element.66.mixes, f32[2,4,2,384,256]{4,3,2,1,0:T(8,128)S(1)} %get-tuple-element.73.turns, bf16[8,128,128]{2,1,0:T(8,128)(2,1)S(1)} %pad_maximum_fusion.1.refs_0_, ...), custom_call_target="tpu_custom_call" | custom-call | flops 1207959552 | bytes 1572864 | tf_op jit(solution)/shard_map/merge_near/pallas_call | solution.py:531
  56.1 0.0 collective-permute-done.11.refs_2_
  56.1 0.6 collective-permute-start.18
  56.7 0.8 %collective-permute-start.19 = (bf16[4,128,128]{2,1,0:T(8,128)(2,1)S(1)}, bf16[4,128,128]{2,1,0:T(8,128)(2,1)S(1)}, u32[]{:S(2)}, u32[]{:S(2)}) collective-permute-start(bf16[4,128,128]{2,1,0:T(8,128)(2,1)S(1)} %slice.53), channel_id=1, source_target_pairs={{0,16},{8,24},{16,0},{24,8},{1,17},{9,25},{17,1},{25,9},{2,18},{10... | collective-permute-start | bytes 393224 | tf_op jit(solution)/shard_map/ppermute | solution.py:590
  57.5 1.4 %merge_near.5 = (bf16[2,1,384,512]{3,2,1,0:T(8,128)(2,1)S(1)}, f32[2,1,2,384,256]{4,3,2,1,0:T(8,128)S(1)}) custom-call(bf16[4,768,256]{2,1,0:T(8,128)(2,1)S(1)} %get-tuple-element.66.mixes, f32[2,4,2,384,256]{4,3,2,1,0:T(8,128)S(1)} %get-tuple-element.68.turns, bf16[8,128,128]{2,1,0:T(8,128)(2,1)S(1)} %pad_maximum_fusion.refs_0_, ...), custom_call_target="tpu_custom_call" | custom-call | flops 1207959552 | bytes 1572864 | tf_op jit(solution)/shard_map/merge_near/pallas_call | solution.py:531
  59.0 0.0 collective-permute-done.20.refs_0_
  59.0 0.0 collective-permute-done.21.refs_1_
  59.0 2.8 %merge_far.4.refs_2_ = f32[384,24,128]{2,1,0:T(8,128)} custom-call(bf16[4,768,256]{2,1,0:T(8,128)(2,1)S(1)} %get-tuple-element.66.mixes, bf16[4,384,384]{2,1,0:T(8,128)(2,1)S(1)} %get-tuple-element.67.mats, f32[2,4,2,384,256]{4,3,2,1,0:T(8,128)S(1)} %get-tuple-element.73.turns, ...), custom_call_target="tpu_custom_call", output_to_operand_aliasing={{}: (7, {})} | custom-call | flops 1207959552 | bytes 3145728 | tf_op jit(solution)/shard_map/merge_far/pallas_call | solution.py:566
  61.8 0.0 collective-permute-done.18.refs_0_
  61.8 2.8 %merge_far.5 = f32[384,24,128]{2,1,0:T(8,128)} custom-call(bf16[4,768,256]{2,1,0:T(8,128)(2,1)S(1)} %get-tuple-element.66.mixes, bf16[4,384,384]{2,1,0:T(8,128)(2,1)S(1)} %get-tuple-element.67.mats, f32[2,4,2,384,256]{4,3,2,1,0:T(8,128)S(1)} %get-tuple-element.68.turns, ...), custom_call_target="tpu_custom_call", output_to_operand_aliasing={{}: (7, {})} | custom-call | flops 1207959552 | bytes 3145728 | tf_op jit(solution)/shard_map/merge_far/pallas_call | solution.py:566
  (23 shorter events, 0.2 us)
Async XLA Ops:
  7.2 3.6 %collective-permute-start = (bf16[4,384,128]{2,1,0:T(8,128)(2,1)}, bf16[4,384,128]{2,1,0:T(8,128)(2,1)S(1)}, u32[]{:S(2)}, u32[]{:S(2)}) collective-permute-start(bf16[4,384,128]{2,1,0:T(8,128)(2,1)} %get-tuple-element.47), channel_id=1, source_target_pairs={{0,1},{1,0},{2,3},{3,2},{4,5},{5,4},{6,7},{7,6},{8,9},{9,8},{10,11... | collective-permute-start | bytes 1179656 | tf_op jit(solution)/shard_map/ppermute | solution.py:590
  7.3 16.2 %collective-permute-start.4 = (bf16[912,128]{1,0:T(8,128)(2,1)}, bf16[912,128]{1,0:T(8,128)(2,1)S(1)}, u32[]{:S(2)}, u32[]{:S(2)}) collective-permute-start(bf16[912,128]{1,0:T(8,128)(2,1)} %get-tuple-element.57.refs_0_), channel_id=1, source_target_pairs={{0,8},{8,0},{16,24},{24,16},{1,9},{9,1},{17,25},{25,17},{2,10},{10... | collective-permute-start | bytes 700424 | tf_op jit(solution)/shard_map/ppermute | solution.py:590
  8.8 17.1 %collective-permute-start.5 = (bf16[912,128]{1,0:T(8,128)(2,1)}, bf16[912,128]{1,0:T(8,128)(2,1)S(1)}, u32[]{:S(2)}, u32[]{:S(2)}) collective-permute-start(bf16[912,128]{1,0:T(8,128)(2,1)} %get-tuple-element.57.refs_0_), channel_id=1, source_target_pairs={{0,16},{8,24},{16,0},{24,8},{1,17},{9,25},{17,1},{25,9},{2,18},{10... | collective-permute-start | bytes 700424 | tf_op jit(solution)/shard_map/ppermute | solution.py:590
  10.3 17.0 %collective-permute-start.6 = (bf16[912,128]{1,0:T(8,128)(2,1)}, bf16[912,128]{1,0:T(8,128)(2,1)S(1)}, u32[]{:S(2)}, u32[]{:S(2)}) collective-permute-start(bf16[912,128]{1,0:T(8,128)(2,1)} %get-tuple-element.57.refs_0_), channel_id=1, source_target_pairs={{0,24},{8,16},{16,8},{24,0},{1,25},{9,17},{17,9},{25,1},{2,26},{10... | collective-permute-start | bytes 700424 | tf_op jit(solution)/shard_map/ppermute | solution.py:590
  10.8 1.0 %copy-start = (bf16[4,384,128]{2,1,0:T(8,128)(2,1)S(1)}, bf16[4,384,128]{2,1,0:T(8,128)(2,1)}, u32[]{:S(2)}) copy-start(bf16[4,384,128]{2,1,0:T(8,128)(2,1)} %get-tuple-element.46.refs_0_) | copy-start | bytes 1179652
  11.9 4.4 %collective-permute-start.7 = (bf16[2,128,128]{2,1,0:T(8,128)(2,1)S(1)}, bf16[2,128,128]{2,1,0:T(8,128)(2,1)S(1)}, u32[]{:S(2)}, u32[]{:S(2)}) collective-permute-start(bf16[2,128,128]{2,1,0:T(8,128)(2,1)S(1)} %get-tuple-element.54), channel_id=1, source_target_pairs={{0,2},{1,3},{2,0},{3,1},{4,6},{5,7},{6,4},{7,5},{8,10},{9,11},{10,... | collective-permute-start | bytes 196616 | tf_op jit(solution)/shard_map/ppermute | solution.py:590
  13.5 5.3 %collective-permute-start.8 = (bf16[2,128,128]{2,1,0:T(8,128)(2,1)S(1)}, bf16[2,128,128]{2,1,0:T(8,128)(2,1)S(1)}, u32[]{:S(2)}, u32[]{:S(2)}) collective-permute-start(bf16[2,128,128]{2,1,0:T(8,128)(2,1)S(1)} %get-tuple-element.55), channel_id=1, source_target_pairs={{0,4},{1,5},{2,6},{3,7},{4,0},{5,1},{6,2},{7,3},{8,12},{9,13},{10,... | collective-permute-start | bytes 196616 | tf_op jit(solution)/shard_map/ppermute | solution.py:590
  16.2 4.6 %collective-permute-start.9 = (bf16[2,128,128]{2,1,0:T(8,128)(2,1)S(1)}, bf16[2,128,128]{2,1,0:T(8,128)(2,1)S(1)}, u32[]{:S(2)}, u32[]{:S(2)}) collective-permute-start(bf16[2,128,128]{2,1,0:T(8,128)(2,1)S(1)} %get-tuple-element.56), channel_id=1, source_target_pairs={{0,6},{1,7},{2,4},{3,5},{4,2},{5,3},{6,0},{7,1},{8,14},{9,15},{10,... | collective-permute-start | bytes 196616 | tf_op jit(solution)/shard_map/ppermute | solution.py:590
  18.8 16.1 %collective-permute-start.1 = (bf16[2,256,128]{2,1,0:T(8,128)(2,1)S(1)}, bf16[2,256,128]{2,1,0:T(8,128)(2,1)S(1)}, u32[]{:S(2)}, u32[]{:S(2)}) collective-permute-start(bf16[2,256,128]{2,1,0:T(8,128)(2,1)S(1)} %get-tuple-element.49), channel_id=1, source_target_pairs={{0,2},{1,3},{2,0},{3,1},{4,6},{5,7},{6,4},{7,5},{8,10},{9,11},{10,... | collective-permute-start | bytes 393224 | tf_op jit(solution)/shard_map/ppermute | solution.py:590
  20.8 14.1 %collective-permute-start.2 = (bf16[2,256,128]{2,1,0:T(8,128)(2,1)S(1)}, bf16[2,256,128]{2,1,0:T(8,128)(2,1)S(1)}, u32[]{:S(2)}, u32[]{:S(2)}) collective-permute-start(bf16[2,256,128]{2,1,0:T(8,128)(2,1)S(1)} %get-tuple-element.50), channel_id=1, source_target_pairs={{0,4},{1,5},{2,6},{3,7},{4,0},{5,1},{6,2},{7,3},{8,12},{9,13},{10,... | collective-permute-start | bytes 393224 | tf_op jit(solution)/shard_map/ppermute | solution.py:590
  23.5 11.4 %collective-permute-start.3 = (bf16[2,256,128]{2,1,0:T(8,128)(2,1)S(1)}, bf16[2,256,128]{2,1,0:T(8,128)(2,1)S(1)}, u32[]{:S(2)}, u32[]{:S(2)}) collective-permute-start(bf16[2,256,128]{2,1,0:T(8,128)(2,1)S(1)} %get-tuple-element.51), channel_id=1, source_target_pairs={{0,6},{1,7},{2,4},{3,5},{4,2},{5,3},{6,0},{7,1},{8,14},{9,15},{10,... | collective-permute-start | bytes 393224 | tf_op jit(solution)/shard_map/ppermute | solution.py:590
  25.9 12.3 %collective-permute-start.14 = (bf16[8,128,128]{2,1,0:T(8,128)(2,1)S(1)}, bf16[8,128,128]{2,1,0:T(8,128)(2,1)S(1)}, u32[]{:S(2)}, u32[]{:S(2)}) collective-permute-start(bf16[8,128,128]{2,1,0:T(8,128)(2,1)S(1)} %constant_dynamic-update-slice_fusion.refs_0_), channel_id=1, source_target_pairs={{0,8},{8,0},{16,24},{24,16},{1,9},{9,1},{17,25},{25,17},{2,10},{10... | collective-permute-start | bytes 786440 | tf_op jit(solution)/shard_map/ppermute | solution.py:590
  27.4 7.6 %collective-permute-start.15 = (bf16[8,128,128]{2,1,0:T(8,128)(2,1)S(1)}, bf16[8,128,128]{2,1,0:T(8,128)(2,1)S(1)}, u32[]{:S(2)}, u32[]{:S(2)}) collective-permute-start(bf16[8,128,128]{2,1,0:T(8,128)(2,1)S(1)} %constant_dynamic-update-slice_fusion.refs_0_), channel_id=1, source_target_pairs={{0,16},{8,24},{16,0},{24,8},{1,17},{9,25},{17,1},{25,9},{2,18},{10... | collective-permute-start | bytes 786440 | tf_op jit(solution)/shard_map/ppermute | solution.py:590
  28.9 0.9 %copy-start.1 = (bf16[912,128]{1,0:T(8,128)(2,1)S(1)}, bf16[912,128]{1,0:T(8,128)(2,1)}, u32[]{:S(2)}) copy-start(bf16[912,128]{1,0:T(8,128)(2,1)} %get-tuple-element.57.refs_0_) | copy-start | bytes 700420
  35.0 6.4 %collective-permute-start.16 = (bf16[4,128,128]{2,1,0:T(8,128)(2,1)S(1)}, bf16[4,128,128]{2,1,0:T(8,128)(2,1)S(1)}, u32[]{:S(2)}, u32[]{:S(2)}) collective-permute-start(bf16[4,128,128]{2,1,0:T(8,128)(2,1)S(1)} %slice.56), channel_id=1, source_target_pairs={{0,8},{8,0},{16,24},{24,16},{1,9},{9,1},{17,25},{25,17},{2,10},{10... | collective-permute-start | bytes 393224 | tf_op jit(solution)/shard_map/ppermute | solution.py:590
  36.1 15.6 %collective-permute-start.12 = (bf16[8,128,128]{2,1,0:T(8,128)(2,1)S(1)}, bf16[8,128,128]{2,1,0:T(8,128)(2,1)S(1)}, u32[]{:S(2)}, u32[]{:S(2)}) collective-permute-start(bf16[8,128,128]{2,1,0:T(8,128)(2,1)S(1)} %pad_maximum_fusion.1.refs_0_), channel_id=1, source_target_pairs={{0,8},{8,0},{16,24},{24,16},{1,9},{9,1},{17,25},{25,17},{2,10},{10... | collective-permute-start | bytes 786440 | tf_op jit(solution)/shard_map/ppermute | solution.py:590
  37.2 14.5 %collective-permute-start.13 = (bf16[8,128,128]{2,1,0:T(8,128)(2,1)S(1)}, bf16[8,128,128]{2,1,0:T(8,128)(2,1)S(1)}, u32[]{:S(2)}, u32[]{:S(2)}) collective-permute-start(bf16[8,128,128]{2,1,0:T(8,128)(2,1)S(1)} %pad_maximum_fusion.1.refs_0_), channel_id=1, source_target_pairs={{0,16},{8,24},{16,0},{24,8},{1,17},{9,25},{17,1},{25,9},{2,18},{10... | collective-permute-start | bytes 786440 | tf_op jit(solution)/shard_map/ppermute | solution.py:590
  38.2 10.7 %collective-permute-start.17 = (bf16[4,128,128]{2,1,0:T(8,128)(2,1)S(1)}, bf16[4,128,128]{2,1,0:T(8,128)(2,1)S(1)}, u32[]{:S(2)}, u32[]{:S(2)}) collective-permute-start(bf16[4,128,128]{2,1,0:T(8,128)(2,1)S(1)} %slice.57), channel_id=1, source_target_pairs={{0,16},{8,24},{16,0},{24,8},{1,17},{9,25},{17,1},{25,9},{2,18},{10... | collective-permute-start | bytes 393224 | tf_op jit(solution)/shard_map/ppermute | solution.py:590
  39.3 16.7 %collective-permute-start.10 = (bf16[8,128,128]{2,1,0:T(8,128)(2,1)S(1)}, bf16[8,128,128]{2,1,0:T(8,128)(2,1)S(1)}, u32[]{:S(2)}, u32[]{:S(2)}) collective-permute-start(bf16[8,128,128]{2,1,0:T(8,128)(2,1)S(1)} %pad_maximum_fusion.refs_0_), channel_id=1, source_target_pairs={{0,8},{8,0},{16,24},{24,16},{1,9},{9,1},{17,25},{25,17},{2,10},{10... | collective-permute-start | bytes 786440 | tf_op jit(solution)/shard_map/ppermute | solution.py:590
  41.4 14.6 %collective-permute-start.11 = (bf16[8,128,128]{2,1,0:T(8,128)(2,1)S(1)}, bf16[8,128,128]{2,1,0:T(8,128)(2,1)S(1)}, u32[]{:S(2)}, u32[]{:S(2)}) collective-permute-start(bf16[8,128,128]{2,1,0:T(8,128)(2,1)S(1)} %pad_maximum_fusion.refs_0_), channel_id=1, source_target_pairs={{0,16},{8,24},{16,0},{24,8},{1,17},{9,25},{17,1},{25,9},{2,18},{10... | collective-permute-start | bytes 786440 | tf_op jit(solution)/shard_map/ppermute | solution.py:590
  51.7 7.3 %collective-permute-start.20 = (bf16[4,128,128]{2,1,0:T(8,128)(2,1)S(1)}, bf16[4,128,128]{2,1,0:T(8,128)(2,1)S(1)}, u32[]{:S(2)}, u32[]{:S(2)}) collective-permute-start(bf16[4,128,128]{2,1,0:T(8,128)(2,1)S(1)} %slice.54), channel_id=1, source_target_pairs={{0,8},{8,0},{16,24},{24,16},{1,9},{9,1},{17,25},{25,17},{2,10},{10... | collective-permute-start | bytes 393224 | tf_op jit(solution)/shard_map/ppermute | solution.py:590
  53.0 6.0 %collective-permute-start.21 = (bf16[4,128,128]{2,1,0:T(8,128)(2,1)S(1)}, bf16[4,128,128]{2,1,0:T(8,128)(2,1)S(1)}, u32[]{:S(2)}, u32[]{:S(2)}) collective-permute-start(bf16[4,128,128]{2,1,0:T(8,128)(2,1)S(1)} %slice.55), channel_id=1, source_target_pairs={{0,16},{8,24},{16,0},{24,8},{1,17},{9,25},{17,1},{25,9},{2,18},{10... | collective-permute-start | bytes 393224 | tf_op jit(solution)/shard_map/ppermute | solution.py:590
  56.1 5.7 %collective-permute-start.18 = (bf16[4,128,128]{2,1,0:T(8,128)(2,1)S(1)}, bf16[4,128,128]{2,1,0:T(8,128)(2,1)S(1)}, u32[]{:S(2)}, u32[]{:S(2)}) collective-permute-start(bf16[4,128,128]{2,1,0:T(8,128)(2,1)S(1)} %slice.52), channel_id=1, source_target_pairs={{0,8},{8,0},{16,24},{24,16},{1,9},{9,1},{17,25},{25,17},{2,10},{10... | collective-permute-start | bytes 393224 | tf_op jit(solution)/shard_map/ppermute | solution.py:590
  56.7 5.1 %collective-permute-start.19 = (bf16[4,128,128]{2,1,0:T(8,128)(2,1)S(1)}, bf16[4,128,128]{2,1,0:T(8,128)(2,1)S(1)}, u32[]{:S(2)}, u32[]{:S(2)}) collective-permute-start(bf16[4,128,128]{2,1,0:T(8,128)(2,1)S(1)} %slice.53), channel_id=1, source_target_pairs={{0,16},{8,24},{16,0},{24,8},{1,17},{9,25},{17,1},{25,9},{2,18},{10... | collective-permute-start | bytes 393224 | tf_op jit(solution)/shard_map/ppermute | solution.py:590
where the time goes:
time: 65.9 us; the launch traced here: 64.6 us
  starting transfers between devices  25.2 us (38%)
  Pallas kernels  24.9 us (38%)
  waiting for transfers between devices  12.1 us (18%)
  local copies, waits for them, and re-layouts  2.08 us (3%)
    ppermute x22, starting transfers between devices, hop(): lax.ppermute(value, axis, [(i, i ^ offset) for i in range(lax.axis_size(a...  25.2 us
    ppermute x22, waiting for transfers between devices, hop(): lax.ppermute(value, axis, [(i, i ^ offset) for i in range(lax.axis_size(a...  12.1 us
    pallas_call x3, Pallas kernels, merge_far(): pl.pallas_call(functools.partial(far_kernel, groups, (high - low) // pair...  8.4 us
    pallas_call x1, Pallas kernels, compress(): pl.pallas_call(functools.partial(compress_kernel, ranks), out_shape=[jax....  7.18 us
    pallas_call x1, Pallas kernels, prepare(): pl.pallas_call(functools.partial(prepare_kernel, groups, ranks, rows, sam...  5.03 us
    pallas_call x3, Pallas kernels, merge_near(): pl.pallas_call(functools.partial(near_kernel, groups, count, held), out_s...  4.28 us
    unnamed x7, local copies, waits for them, and re-layouts  1.97 us
  transfers between devices with their start and end apart: 22, of which 5 were waited for; matrix products, arithmetic and copies ran while one was open for 0% of the time, Pallas kernels for 23%

commit v1 on v0

--- a/solution.py
+++ b/solution.py
@@ -133,9 +133,9 @@
 
 
 def compress_kernel(ranks, me_ref, shifts_ref, *refs):
-    loads, (near, odd, early) = refs[:LOADS], refs[LOADS : LOADS + 3]
-    total, filt_ref, *held = refs[LOADS + 3 : -1]
-    done = refs[-1]
+    loads, (near_out, odd_out, early_out) = refs[:LOADS], refs[LOADS : LOADS + 3]
+    total, filt_ref, near, odd, early, *held = refs[LOADS + 3 : -2]
+    done, sent = refs[-2:]
     echo_ref, first_ref, twiddle_ref, raw_ref, forward_ref, backward_ref, last_ref = held[:7]
     taps_ref, offsets_ref, rates_ref = held[7:]
     held = [*held, early.at[pl.ds(0, loads[-1].shape[0])]]
@@ -176,6 +176,8 @@
         copy.wait()
     load_filter(raw_ref, filt_ref)
     encode(early, loads[-1].shape[0], taps_ref, offsets_ref, rates_ref)
+    sends = [pltpu.make_async_copy(early, early_out, sent.at[ranks])]
+    sends[0].start()
     z = dot_table(jnp.concatenate(sections, axis=0), forward_ref, PASSES[1])
     sections = []
     for q in range(pulses):
@@ -201,10 +203,14 @@
             total[pl.ds(part * pulses + q, radix, stride=wide), :] = moved
 
     length = radix // ranks * wide
-    for d in range(ranks):
+    for d in (*range(1, ranks, 2), *range(0, ranks, 2)):
         start = pl.multiple_of(lax.bitwise_xor(me, d) * length, 8)
-        target = odd if d % 2 else near
-        target[d // 2] = total[pl.ds(start, length), :].astype(BF16)
+        staged, target = (odd, odd_out) if d % 2 else (near, near_out)
+        staged[d // 2] = total[pl.ds(start, length), :].astype(BF16)
+        sends.append(pltpu.make_async_copy(staged.at[d // 2], target.at[d // 2], sent.at[d]))
+        sends[-1].start()
+    for copy in sends:
+        copy.wait()
 
 
 def compress(echoes, filter_spectrum, range_shifts, steering, tap_offsets, tap_weights, phase_rates, me, ranks):
@@ -230,10 +236,12 @@
         ]
         + [jax.ShapeDtypeStruct((2 * angles + 48 * angles // LANES, steer.shape[1]), BF16)],
         in_specs=[smem, smem] + [away] * LOADS,
-        out_specs=[vmem] * 3,
+        out_specs=[away] * 3,
         scratch_shapes=[pltpu.VMEM((radix * wide, LANES), F32), pltpu.VMEM((2, radix, LANES), F32)]
+        + [pltpu.VMEM((half, radix // ranks * wide, LANES), BF16) for _ in range(2)]
+        + [pltpu.VMEM((2 * angles + 48 * angles // LANES, steer.shape[1]), BF16)]
         + [pltpu.VMEM(x.shape, x.dtype) for x in loads[:-1]]
-        + [pltpu.SemaphoreType.DMA((LOADS + pulses // QUAD,))],
+        + [pltpu.SemaphoreType.DMA((LOADS + pulses // QUAD,)), pltpu.SemaphoreType.DMA((ranks + 1,))],
         compiler_params=pltpu.CompilerParams(vmem_limit_bytes=COMPRESS_LIMIT),
         cost_estimate=pl.CostEstimate(
             flops=pulses * samples * 4000, bytes_accessed=pulses * samples * 12, transcendentals=0
@@ -279,10 +287,9 @@
     return a[0] * b[0] - a[1] * b[1], a[0] * b[1] + a[1] * b[0]
 
 
-def prepare_kernel(groups, ranks, rows, samples, pair, cuts, me_ref, *refs):
+def prepare_kernel(groups, ranks, rows, samples, pair, me_ref, *refs):
     steer = refs[:groups]
-    mixes, mats, *turns = refs[groups:]
-    places = [(cut, at) for cut, (low, high) in enumerate(cuts) for at in range((high - low) // pair)]
+    mixes, mats, strides, turns = refs[groups:]
     angles = mats.shape[-1]
     members = steer[0].shape[-1]
     me = me_ref[0]
@@ -340,10 +347,41 @@
                     first = complex_times(first, step)
                 now = first
                 jump = (spread(5, n), spread(6, n))
-                for index, (cut, at) in enumerate(places):
-                    if index:
+                for at in range(turns.shape[0]):
+                    if at:
                         now = complex_times(now, jump)
-                    turns[cut][at, n, 0, :, here], turns[cut][at, n, 1, :, here] = now
+                    turns[at, n, 0, :, here], turns[at, n, 1, :, here] = now
+            strides[n, 0], strides[n, 1] = jump
+
+
+def spin_kernel(strides, start, *turns):
+    last, groups, _, angles, side = start.shape
+    for n in range(groups):
+        for top in range(0, angles, BAND):
+            band = slice(top, top + BAND)
+            jump = (strides[n, 0, band], strides[n, 1, band])
+            for at in range(0, side, LANES):
+                here = slice(at, at + LANES)
+                now = (start[last - 1, n, 0, band, here], start[last - 1, n, 1, band, here])
+                for turn in turns:
+                    for place in range(last):
+                        now = complex_times(now, jump)
+                        turn[place, n, 0, band, here], turn[place, n, 1, band, here] = now
+
+
+def spin(strides, start, count):
+    vmem = pl.BlockSpec(memory_space=pltpu.VMEM)
+    return pl.pallas_call(
+        spin_kernel,
+        out_shape=[jax.ShapeDtypeStruct(start.shape, F32)] * count,
+        in_specs=[vmem] * 2,
+        out_specs=[vmem] * count,
+        compiler_params=pltpu.CompilerParams(vmem_limit_bytes=MERGE_LIMIT),
+        cost_estimate=pl.CostEstimate(
+            flops=6 * count * start.size, bytes_accessed=4 * start.size, transcendentals=0
+        ),
+        name="spin",
+    )(strides, start)
 
 
 def small_turn(x):
@@ -352,22 +390,20 @@
     return cosine, x * (1.0 - y * (1.0 / 6.0 - y * (1.0 / 120.0 - y * (1.0 / 5040.0))))
 
 
-def prepare(steer, angles, me, groups, ranks, rows, samples, pair, cuts):
+def prepare(steer, angles, me, groups, ranks, rows, samples, pair, unit):
     members = steer[0].shape[1]
     smem = pl.BlockSpec(memory_space=pltpu.SMEM)
     vmem = pl.BlockSpec(memory_space=pltpu.VMEM)
     return pl.pallas_call(
-        functools.partial(prepare_kernel, groups, ranks, rows, samples, pair, cuts),
+        functools.partial(prepare_kernel, groups, ranks, rows, samples, pair),
         out_shape=[
             jax.ShapeDtypeStruct((groups, 2 * angles, 2 * members), BF16),
             jax.ShapeDtypeStruct((groups, angles, angles), BF16),
-        ]
-        + [
-            jax.ShapeDtypeStruct(((high - low) // pair, groups, 2, angles, pair * LANES), F32)
-            for low, high in cuts
+            jax.ShapeDtypeStruct((groups, 2, angles, LANES), F32),
+            jax.ShapeDtypeStruct((unit // pair, groups, 2, angles, pair * LANES), F32),
         ],
         in_specs=[smem] + [vmem] * len(steer),
-        out_specs=[vmem] * (2 + len(cuts)),
+        out_specs=[vmem] * 4,
         compiler_params=pltpu.CompilerParams(vmem_limit_bytes=32 * 1024 * 1024),
         cost_estimate=pl.CostEstimate(
             flops=groups * angles * members * 40000, bytes_accessed=8 << 20, transcendentals=0
@@ -636,13 +672,13 @@
     arrived = [jnp.concatenate(batch[0], axis=0)]
     steers, _ = lax.optimization_barrier((steers, arrived[0]))
     pair = 2 if unit % 2 == 0 else 1
-    ready = prepare(steers, angles, me, groups, ranks, rows, samples, pair, cuts)
+    ready = prepare(steers, angles, me, groups, ranks, rows, samples, pair, unit)
     if len(batch) > 1:
         batch[1], ready = lax.optimization_barrier((batch[1], ready))
         for at in range(0, batch[1][0].shape[1], unit * wide):
             pieces = [piece[:, at : at + unit * wide] for piece in batch[1]]
             arrived.append(jnp.concatenate(pieces, axis=0))
-    mixes, mats, *turns = ready
+    mixes, mats, strides, *turns = ready
 
     nears = []
     for x in arrived:
@@ -657,7 +693,9 @@
             nears[cut + 1], image = lax.optimization_barrier((nears[cut + 1], image))
         out = merge_far(far, mixes, mats, turns[cut], image, partial, rows, low, high, unit, out)
         if not cut and len(cuts) > 1:
-            nears[1], out = lax.optimization_barrier((nears[1], out))
+            strides, out = lax.optimization_barrier((strides, out))
+            turns += spin(strides, turns[0], len(cuts) - 1)
+            nears[1], turns[1], out = lax.optimization_barrier((nears[1], turns[1], out))
     out = out.reshape(angles, rows, 2, LANES).transpose(0, 2, 1, 3)
     out = with_layout_constraint(out, Layout(major_to_minor=(0, 2, 1, 3)))
     return out.reshape(angles, 2, rows * LANES)

time: 65.9 us -> 66 us (level); the launches traced: 64.6 us -> 65.8 us
  starting transfers between devices: 25.2 us -> 26.3 us
    pallas_call x0 -> x1, Pallas kernels: none -> 1.34 us  [spin(): pl.pallas_call(spin_kernel, out_shape=[jax.ShapeDtypeStruct(start.shape,...]
    pallas_call x1, Pallas kernels: 5.03 us -> 3.8 us  [prepare(): pl.pallas_call(functools.partial(prepare_kernel, groups, ranks, rows, sam...]
    ppermute x22, starting transfers between devices: 25.2 us -> 26.3 us  [hop(): lax.ppermute(value, axis, [(i, i ^ offset) for i in range(lax.axis_size(a...]
  transfers between devices with their start and end apart: 22 -> 22, of which waited for: 5 -> 7; matrix products, arithmetic and copies ran while one was open for 0% -> 0% of each run, Pallas kernels for 23% -> 23%
where the time goes in v1:
time: 66 us; the launch traced here: 65.8 us
  starting transfers between devices  26.3 us (40%)
  Pallas kernels  24.8 us (38%)
  waiting for transfers between devices  12.3 us (19%)
  local copies, waits for them, and re-layouts  2.08 us (3%)
    ppermute x22, starting transfers between devices, hop(): lax.ppermute(value, axis, [(i, i ^ offset) for i in range(lax.axis_size(a...  26.3 us
    ppermute x22, waiting for transfers between devices, hop(): lax.ppermute(value, axis, [(i, i ^ offset) for i in range(lax.axis_size(a...  12.3 us
    pallas_call x3, Pallas kernels, merge_far(): pl.pallas_call(functools.partial(far_kernel, groups, (high - low) // pair...  8.31 us
    pallas_call x1, Pallas kernels, compress(): pl.pallas_call(functools.partial(compress_kernel, ranks), out_shape=[jax....  7.13 us
    pallas_call x3, Pallas kernels, merge_near(): pl.pallas_call(functools.partial(near_kernel, groups, count, held), out_s...  4.19 us
    pallas_call x1, Pallas kernels, prepare(): pl.pallas_call(functools.partial(prepare_kernel, groups, ranks, rows, sam...  3.8 us
    unnamed x7, local copies, waits for them, and re-layouts  1.97 us
    pallas_call x1, Pallas kernels, spin(): pl.pallas_call(spin_kernel, out_shape=[jax.ShapeDtypeStruct(start.shape,...  1.34 us
  transfers between devices with their start and end apart: 22, of which 7 were waited for; matrix products, arithmetic and copies ran while one was open for 0% of the time, Pallas kernels for 23%

profile of v1, /device:TPU:16, one launch (start us, length us, event | category | flops | bytes accessed | tf_op | source)
XLA Modules:
  0.0 65.8 jit_solution(758797055761618049)
XLA Ops:
  0.0 7.1 %compress.1 = (bf16[4,384,128]{2,1,0:T(8,128)(2,1)}, bf16[4,384,128]{2,1,0:T(8,128)(2,1)}, bf16[912,128]{1,0:T(8,128)(2,1)}) custom-call(s32[1]{0:T(128)} %bitcast.me_ref, s32[128]{0:T(128)} %shifts_ref.1, f32[16,192,128]{2,1,0:T(8,128)} %bitcast.17, bf16[2,192,192]{2,1,0:T(8,128)(2,1)} %constant.14.clone.refs_1_, f32[2,96,128]{2,1,0:T(8,128)} %constant.18.clone.refs_2_, ...), custom_call_target="tpu_custom_call" | custom-call | flops 786432000 | bytes 2359296 | tf_op jit(solution)/shard_map/compress/pallas_call | solution.py:232
  7.1 0.1 collective-permute-start
  7.2 1.6 %collective-permute-start.4 = (bf16[912,128]{1,0:T(8,128)(2,1)}, bf16[912,128]{1,0:T(8,128)(2,1)S(1)}, u32[]{:S(2)}, u32[]{:S(2)}) collective-permute-start(bf16[912,128]{1,0:T(8,128)(2,1)} %get-tuple-element.60.refs_0_), channel_id=1, source_target_pairs={{0,8},{8,0},{16,24},{24,16},{1,9},{9,1},{17,25},{25,17},{2,10},{10... | collective-permute-start | bytes 700424 | tf_op jit(solution)/shard_map/ppermute | solution.py:626
  8.8 1.5 %collective-permute-start.5 = (bf16[912,128]{1,0:T(8,128)(2,1)}, bf16[912,128]{1,0:T(8,128)(2,1)S(1)}, u32[]{:S(2)}, u32[]{:S(2)}) collective-permute-start(bf16[912,128]{1,0:T(8,128)(2,1)} %get-tuple-element.60.refs_0_), channel_id=1, source_target_pairs={{0,16},{8,24},{16,0},{24,8},{1,17},{9,25},{17,1},{25,9},{2,18},{10... | collective-permute-start | bytes 700424 | tf_op jit(solution)/shard_map/ppermute | solution.py:626
  10.3 0.5 collective-permute-start.6
  10.8 0.0 collective-permute-done.refs_1_
  10.8 1.0 %copy-done = bf16[4,384,128]{2,1,0:T(8,128)(2,1)S(1)} copy-done((bf16[4,384,128]{2,1,0:T(8,128)(2,1)S(1)}, bf16[4,384,128]{2,1,0:T(8,128)(2,1)}, u32[]{:S(2)}) %copy-start) | copy-done | bytes 393240
  11.8 0.1 pack.1
  11.8 1.6 %collective-permute-start.7 = (bf16[2,128,128]{2,1,0:T(8,128)(2,1)S(1)}, bf16[2,128,128]{2,1,0:T(8,128)(2,1)S(1)}, u32[]{:S(2)}, u32[]{:S(2)}) collective-permute-start(bf16[2,128,128]{2,1,0:T(8,128)(2,1)S(1)} %get-tuple-element.57), channel_id=1, source_target_pairs={{0,2},{1,3},{2,0},{3,1},{4,6},{5,7},{6,4},{7,5},{8,10},{9,11},{10,... | collective-permute-start | bytes 196616 | tf_op jit(solution)/shard_map/ppermute | solution.py:626
  13.5 0.3 collective-permute-start.8
  13.8 2.4 %collective-permute-done.7 = bf16[2,128,128]{2,1,0:T(8,128)(2,1)S(1)} collective-permute-done((bf16[2,128,128]{2,1,0:T(8,128)(2,1)S(1)}, bf16[2,128,128]{2,1,0:T(8,128)(2,1)S(1)}, u32[]{:S(2)}, u32[]{:S(2)}) %collective-permute-start.7) | collective-permute-done | bytes 65568 | tf_op jit(solution)/shard_map/ppermute | solution.py:626
  16.2 0.4 collective-permute-start.9
  16.6 2.1 %collective-permute-done.8 = bf16[2,128,128]{2,1,0:T(8,128)(2,1)S(1)} collective-permute-done((bf16[2,128,128]{2,1,0:T(8,128)(2,1)S(1)}, bf16[2,128,128]{2,1,0:T(8,128)(2,1)S(1)}, u32[]{:S(2)}, u32[]{:S(2)}) %collective-permute-start.8) | collective-permute-done | bytes 65568 | tf_op jit(solution)/shard_map/ppermute | solution.py:626
  18.7 0.6 collective-permute-start.1
  19.4 1.5 %collective-permute-done.9 = bf16[2,128,128]{2,1,0:T(8,128)(2,1)S(1)} collective-permute-done((bf16[2,128,128]{2,1,0:T(8,128)(2,1)S(1)}, bf16[2,128,128]{2,1,0:T(8,128)(2,1)S(1)}, u32[]{:S(2)}, u32[]{:S(2)}) %collective-permute-start.9) | collective-permute-done | bytes 65568 | tf_op jit(solution)/shard_map/ppermute | solution.py:626
  20.8 2.6 %collective-permute-start.2 = (bf16[2,256,128]{2,1,0:T(8,128)(2,1)S(1)}, bf16[2,256,128]{2,1,0:T(8,128)(2,1)S(1)}, u32[]{:S(2)}, u32[]{:S(2)}) collective-permute-start(bf16[2,256,128]{2,1,0:T(8,128)(2,1)S(1)} %get-tuple-element.53), channel_id=1, source_target_pairs={{0,4},{1,5},{2,6},{3,7},{4,0},{5,1},{6,2},{7,3},{8,12},{9,13},{10,... | collective-permute-start | bytes 393224 | tf_op jit(solution)/shard_map/ppermute | solution.py:626
  23.4 0.0 collective-permute-done.4.refs_1_
  23.5 2.4 %collective-permute-start.3 = (bf16[2,256,128]{2,1,0:T(8,128)(2,1)S(1)}, bf16[2,256,128]{2,1,0:T(8,128)(2,1)S(1)}, u32[]{:S(2)}, u32[]{:S(2)}) collective-permute-start(bf16[2,256,128]{2,1,0:T(8,128)(2,1)S(1)} %get-tuple-element.54), channel_id=1, source_target_pairs={{0,6},{1,7},{2,4},{3,5},{4,2},{5,3},{6,0},{7,1},{8,14},{9,15},{10,... | collective-permute-start | bytes 393224 | tf_op jit(solution)/shard_map/ppermute | solution.py:626
  25.8 0.0 collective-permute-done.5.refs_2_
  25.9 1.5 %collective-permute-start.10 = (bf16[8,128,128]{2,1,0:T(8,128)(2,1)S(1)}, bf16[8,128,128]{2,1,0:T(8,128)(2,1)S(1)}, u32[]{:S(2)}, u32[]{:S(2)}) collective-permute-start(bf16[8,128,128]{2,1,0:T(8,128)(2,1)S(1)} %constant_dynamic-update-slice_fusion.refs_0_), channel_id=1, source_target_pairs={{0,8},{8,0},{16,24},{24,16},{1,9},{9,1},{17,25},{25,17},{2,10},{10... | collective-permute-start | bytes 786440 | tf_op jit(solution)/shard_map/ppermute | solution.py:626
  27.3 0.0 collective-permute-done.6.refs_3_
  27.4 1.5 %collective-permute-start.11 = (bf16[8,128,128]{2,1,0:T(8,128)(2,1)S(1)}, bf16[8,128,128]{2,1,0:T(8,128)(2,1)S(1)}, u32[]{:S(2)}, u32[]{:S(2)}) collective-permute-start(bf16[8,128,128]{2,1,0:T(8,128)(2,1)S(1)} %constant_dynamic-update-slice_fusion.refs_0_), channel_id=1, source_target_pairs={{0,16},{8,24},{16,0},{24,8},{1,17},{9,25},{17,1},{25,9},{2,18},{10... | collective-permute-start | bytes 786440 | tf_op jit(solution)/shard_map/ppermute | solution.py:626
  28.9 0.9 %copy-done.1 = bf16[912,128]{1,0:T(8,128)(2,1)S(1)} copy-done((bf16[912,128]{1,0:T(8,128)(2,1)S(1)}, bf16[912,128]{1,0:T(8,128)(2,1)}, u32[]{:S(2)}) %copy-start.1) | copy-done | bytes 233496
  29.8 3.8 %prepare.1 = (bf16[4,768,256]{2,1,0:T(8,128)(2,1)S(1)}, bf16[4,384,384]{2,1,0:T(8,128)(2,1)S(1)}, f32[4,2,384,128]{3,2,1,0:T(8,128)S(1)}, f32[2,4,2,384,256]{4,3,2,1,0:T(8,128)S(1)}) custom-call(s32[1]{0:T(128)} %bitcast.me_ref, bf16[912,128]{1,0:T(8,128)(2,1)S(1)} %copy-done.1, bf16[912,128]{1,0:T(8,128)(2,1)S(1)} %collective-permute-done.4.refs_1_, ...), custom_call_target="tpu_custom_call" | custom-call | flops 7864320000 | bytes 8388608 | tf_op jit(solution)/shard_map/prepare/pallas_call | solution.py:397
  33.6 0.0 collective-permute-done.2
  33.6 0.7 %collective-permute-done.3 = bf16[2,256,128]{2,1,0:T(8,128)(2,1)S(1)} collective-permute-done((bf16[2,256,128]{2,1,0:T(8,128)(2,1)S(1)}, bf16[2,256,128]{2,1,0:T(8,128)(2,1)S(1)}, u32[]{:S(2)}, u32[]{:S(2)}) %collective-permute-start.3) | collective-permute-done | bytes 131104 | tf_op jit(solution)/shard_map/ppermute | solution.py:626
  34.4 0.0 collective-permute-done.11.refs_2_
  34.4 1.6 %collective-permute-start.12 = (bf16[4,128,128]{2,1,0:T(8,128)(2,1)S(1)}, bf16[4,128,128]{2,1,0:T(8,128)(2,1)S(1)}, u32[]{:S(2)}, u32[]{:S(2)}) collective-permute-start(bf16[4,128,128]{2,1,0:T(8,128)(2,1)S(1)} %slice.56), channel_id=1, source_target_pairs={{0,8},{8,0},{16,24},{24,16},{1,9},{9,1},{17,25},{25,17},{2,10},{10... | collective-permute-start | bytes 393224 | tf_op jit(solution)/shard_map/ppermute | solution.py:626
  36.0 0.6 collective-permute-start.16
  36.6 1.5 %collective-permute-start.17 = (bf16[8,128,128]{2,1,0:T(8,128)(2,1)S(1)}, bf16[8,128,128]{2,1,0:T(8,128)(2,1)S(1)}, u32[]{:S(2)}, u32[]{:S(2)}) collective-permute-start(bf16[8,128,128]{2,1,0:T(8,128)(2,1)S(1)} %pad_maximum_fusion.1.refs_0_), channel_id=1, source_target_pairs={{0,16},{8,24},{16,0},{24,8},{1,17},{9,25},{17,1},{25,9},{2,18},{10... | collective-permute-start | bytes 786440 | tf_op jit(solution)/shard_map/ppermute | solution.py:626
  38.2 0.6 collective-permute-start.13
  38.8 1.6 %collective-permute-start.14 = (bf16[8,128,128]{2,1,0:T(8,128)(2,1)S(1)}, bf16[8,128,128]{2,1,0:T(8,128)(2,1)S(1)}, u32[]{:S(2)}, u32[]{:S(2)}) collective-permute-start(bf16[8,128,128]{2,1,0:T(8,128)(2,1)S(1)} %pad_maximum_fusion.refs_0_), channel_id=1, source_target_pairs={{0,8},{8,0},{16,24},{24,16},{1,9},{9,1},{17,25},{25,17},{2,10},{10... | collective-permute-start | bytes 786440 | tf_op jit(solution)/shard_map/ppermute | solution.py:626
  40.3 0.5 collective-permute-done.12.refs_0_
  40.9 1.5 %collective-permute-start.15 = (bf16[8,128,128]{2,1,0:T(8,128)(2,1)S(1)}, bf16[8,128,128]{2,1,0:T(8,128)(2,1)S(1)}, u32[]{:S(2)}, u32[]{:S(2)}) collective-permute-start(bf16[8,128,128]{2,1,0:T(8,128)(2,1)S(1)} %pad_maximum_fusion.refs_0_), channel_id=1, source_target_pairs={{0,16},{8,24},{16,0},{24,8},{1,17},{9,25},{17,1},{25,9},{2,18},{10... | collective-permute-start | bytes 786440 | tf_op jit(solution)/shard_map/ppermute | solution.py:626
  42.4 1.4 %merge_near.3 = (bf16[2,1,384,512]{3,2,1,0:T(8,128)(2,1)S(1)}, f32[2,1,2,384,256]{4,3,2,1,0:T(8,128)S(1)}) custom-call(bf16[4,768,256]{2,1,0:T(8,128)(2,1)S(1)} %get-tuple-element.68.mixes, f32[2,4,2,384,256]{4,3,2,1,0:T(8,128)S(1)} %get-tuple-element.71.turns.start, bf16[8,128,128]{2,1,0:T(8,128)(2,1)S(1)} %constant_dynamic-update-slice_fusion.refs_0_, ...), custom_call_target="tpu_custom_call" | custom-call | flops 1207959552 | bytes 1572864 | tf_op jit(solution)/shard_map/merge_near/pallas_call | solution.py:567
  43.8 4.8 %collective-permute-done.13.refs_1_ = bf16[4,128,128]{2,1,0:T(8,128)(2,1)S(1)} collective-permute-done((bf16[4,128,128]{2,1,0:T(8,128)(2,1)S(1)}, bf16[4,128,128]{2,1,0:T(8,128)(2,1)S(1)}, u32[]{:S(2)}, u32[]{:S(2)}) %collective-permute-start.13) | collective-permute-done | bytes 131104 | tf_op jit(solution)/shard_map/ppermute | solution.py:626
  48.6 2.8 %merge_far.3.refs_2_ = f32[384,24,128]{2,1,0:T(8,128)} custom-call(bf16[4,768,256]{2,1,0:T(8,128)(2,1)S(1)} %get-tuple-element.68.mixes, bf16[4,384,384]{2,1,0:T(8,128)(2,1)S(1)} %get-tuple-element.69.mats, f32[2,4,2,384,256]{4,3,2,1,0:T(8,128)S(1)} %get-tuple-element.71.turns.start, bf16[2,1,384,512]{3,2,1,0:T(8,128)(2,1)S(1)} %get-tuple-element.72.image, ...), custom_call_target="tpu_custom_call" | custom-call | flops 1207959552 | bytes 3145728 | tf_op jit(solution)/shard_map/merge_far/pallas_call | solution.py:602
  51.4 1.3 %spin.1 = (f32[2,4,2,384,256]{4,3,2,1,0:T(8,128)S(1)}, f32[2,4,2,384,256]{4,3,2,1,0:T(8,128)S(1)}) custom-call(f32[4,2,384,128]{3,2,1,0:T(8,128)S(1)} %get-tuple-element.74.strides, f32[2,4,2,384,256]{4,3,2,1,0:T(8,128)S(1)} %get-tuple-element.71.turns.start), custom_call_target="tpu_custom_call" | custom-call | flops 18874368 | bytes 6291456 | tf_op jit(solution)/shard_map/spin/pallas_call | solution.py:374
  52.8 0.0 collective-permute-done.16.refs_1_
  52.8 1.6 %collective-permute-start.20 = (bf16[4,128,128]{2,1,0:T(8,128)(2,1)S(1)}, bf16[4,128,128]{2,1,0:T(8,128)(2,1)S(1)}, u32[]{:S(2)}, u32[]{:S(2)}) collective-permute-start(bf16[4,128,128]{2,1,0:T(8,128)(2,1)S(1)} %slice.54), channel_id=1, source_target_pairs={{0,8},{8,0},{16,24},{24,16},{1,9},{9,1},{17,25},{25,17},{2,10},{10... | collective-permute-start | bytes 393224 | tf_op jit(solution)/shard_map/ppermute | solution.py:626
  54.4 1.6 %collective-permute-start.21 = (bf16[4,128,128]{2,1,0:T(8,128)(2,1)S(1)}, bf16[4,128,128]{2,1,0:T(8,128)(2,1)S(1)}, u32[]{:S(2)}, u32[]{:S(2)}) collective-permute-start(bf16[4,128,128]{2,1,0:T(8,128)(2,1)S(1)} %slice.55), channel_id=1, source_target_pairs={{0,16},{8,24},{16,0},{24,8},{1,17},{9,25},{17,1},{25,9},{2,18},{10... | collective-permute-start | bytes 393224 | tf_op jit(solution)/shard_map/ppermute | solution.py:626
  56.0 1.4 %merge_near.4 = (bf16[2,1,384,512]{3,2,1,0:T(8,128)(2,1)S(1)}, f32[2,1,2,384,256]{4,3,2,1,0:T(8,128)S(1)}) custom-call(bf16[4,768,256]{2,1,0:T(8,128)(2,1)S(1)} %get-tuple-element.68.mixes, f32[2,4,2,384,256]{4,3,2,1,0:T(8,128)S(1)} %get-tuple-element.82.turns, bf16[8,128,128]{2,1,0:T(8,128)(2,1)S(1)} %pad_maximum_fusion.1.refs_0_, ...), custom_call_target="tpu_custom_call" | custom-call | flops 1207959552 | bytes 1572864 | tf_op jit(solution)/shard_map/merge_near/pallas_call | solution.py:567
  57.4 0.6 collective-permute-start.18
  58.0 0.6 collective-permute-start.19
  58.6 1.3 %merge_near.5 = (bf16[2,1,384,512]{3,2,1,0:T(8,128)(2,1)S(1)}, f32[2,1,2,384,256]{4,3,2,1,0:T(8,128)S(1)}) custom-call(bf16[4,768,256]{2,1,0:T(8,128)(2,1)S(1)} %get-tuple-element.68.mixes, f32[2,4,2,384,256]{4,3,2,1,0:T(8,128)S(1)} %get-tuple-element.75.turns, bf16[8,128,128]{2,1,0:T(8,128)(2,1)S(1)} %pad_maximum_fusion.refs_0_, ...), custom_call_target="tpu_custom_call" | custom-call | flops 1207959552 | bytes 1572864 | tf_op jit(solution)/shard_map/merge_near/pallas_call | solution.py:567
  60.0 2.8 %merge_far.4.refs_2_ = f32[384,24,128]{2,1,0:T(8,128)} custom-call(bf16[4,768,256]{2,1,0:T(8,128)(2,1)S(1)} %get-tuple-element.68.mixes, bf16[4,384,384]{2,1,0:T(8,128)(2,1)S(1)} %get-tuple-element.69.mats, f32[2,4,2,384,256]{4,3,2,1,0:T(8,128)S(1)} %get-tuple-element.82.turns, ...), custom_call_target="tpu_custom_call", output_to_operand_aliasing={{}: (7, {})} | custom-call | flops 1207959552 | bytes 3145728 | tf_op jit(solution)/shard_map/merge_far/pallas_call | solution.py:602
  62.8 0.3 collective-permute-done.19.refs_1_
  63.1 2.7 %merge_far.5 = f32[384,24,128]{2,1,0:T(8,128)} custom-call(bf16[4,768,256]{2,1,0:T(8,128)(2,1)S(1)} %get-tuple-element.68.mixes, bf16[4,384,384]{2,1,0:T(8,128)(2,1)S(1)} %get-tuple-element.69.mats, f32[2,4,2,384,256]{4,3,2,1,0:T(8,128)S(1)} %get-tuple-element.75.turns, ...), custom_call_target="tpu_custom_call", output_to_operand_aliasing={{}: (7, {})} | custom-call | flops 1207959552 | bytes 3145728 | tf_op jit(solution)/shard_map/merge_far/pallas_call | solution.py:602
  (24 shorter events, 0.2 us)
Async XLA Ops:
  7.1 3.6 %collective-permute-start = (bf16[4,384,128]{2,1,0:T(8,128)(2,1)}, bf16[4,384,128]{2,1,0:T(8,128)(2,1)S(1)}, u32[]{:S(2)}, u32[]{:S(2)}) collective-permute-start(bf16[4,384,128]{2,1,0:T(8,128)(2,1)} %get-tuple-element.50), channel_id=1, source_target_pairs={{0,1},{1,0},{2,3},{3,2},{4,5},{5,4},{6,7},{7,6},{8,9},{9,8},{10,11... | collective-permute-start | bytes 1179656 | tf_op jit(solution)/shard_map/ppermute | solution.py:626
  7.2 16.2 %collective-permute-start.4 = (bf16[912,128]{1,0:T(8,128)(2,1)}, bf16[912,128]{1,0:T(8,128)(2,1)S(1)}, u32[]{:S(2)}, u32[]{:S(2)}) collective-permute-start(bf16[912,128]{1,0:T(8,128)(2,1)} %get-tuple-element.60.refs_0_), channel_id=1, source_target_pairs={{0,8},{8,0},{16,24},{24,16},{1,9},{9,1},{17,25},{25,17},{2,10},{10... | collective-permute-start | bytes 700424 | tf_op jit(solution)/shard_map/ppermute | solution.py:626
  8.8 17.1 %collective-permute-start.5 = (bf16[912,128]{1,0:T(8,128)(2,1)}, bf16[912,128]{1,0:T(8,128)(2,1)S(1)}, u32[]{:S(2)}, u32[]{:S(2)}) collective-permute-start(bf16[912,128]{1,0:T(8,128)(2,1)} %get-tuple-element.60.refs_0_), channel_id=1, source_target_pairs={{0,16},{8,24},{16,0},{24,8},{1,17},{9,25},{17,1},{25,9},{2,18},{10... | collective-permute-start | bytes 700424 | tf_op jit(solution)/shard_map/ppermute | solution.py:626
  10.3 17.1 %collective-permute-start.6 = (bf16[912,128]{1,0:T(8,128)(2,1)}, bf16[912,128]{1,0:T(8,128)(2,1)S(1)}, u32[]{:S(2)}, u32[]{:S(2)}) collective-permute-start(bf16[912,128]{1,0:T(8,128)(2,1)} %get-tuple-element.60.refs_0_), channel_id=1, source_target_pairs={{0,24},{8,16},{16,8},{24,0},{1,25},{9,17},{17,9},{25,1},{2,26},{10... | collective-permute-start | bytes 700424 | tf_op jit(solution)/shard_map/ppermute | solution.py:626
  10.8 1.0 %copy-start = (bf16[4,384,128]{2,1,0:T(8,128)(2,1)S(1)}, bf16[4,384,128]{2,1,0:T(8,128)(2,1)}, u32[]{:S(2)}) copy-start(bf16[4,384,128]{2,1,0:T(8,128)(2,1)} %get-tuple-element.49.refs_0_) | copy-start | bytes 1179652
  11.8 4.4 %collective-permute-start.7 = (bf16[2,128,128]{2,1,0:T(8,128)(2,1)S(1)}, bf16[2,128,128]{2,1,0:T(8,128)(2,1)S(1)}, u32[]{:S(2)}, u32[]{:S(2)}) collective-permute-start(bf16[2,128,128]{2,1,0:T(8,128)(2,1)S(1)} %get-tuple-element.57), channel_id=1, source_target_pairs={{0,2},{1,3},{2,0},{3,1},{4,6},{5,7},{6,4},{7,5},{8,10},{9,11},{10,... | collective-permute-start | bytes 196616 | tf_op jit(solution)/shard_map/ppermute | solution.py:626
  13.5 5.3 %collective-permute-start.8 = (bf16[2,128,128]{2,1,0:T(8,128)(2,1)S(1)}, bf16[2,128,128]{2,1,0:T(8,128)(2,1)S(1)}, u32[]{:S(2)}, u32[]{:S(2)}) collective-permute-start(bf16[2,128,128]{2,1,0:T(8,128)(2,1)S(1)} %get-tuple-element.58), channel_id=1, source_target_pairs={{0,4},{1,5},{2,6},{3,7},{4,0},{5,1},{6,2},{7,3},{8,12},{9,13},{10,... | collective-permute-start | bytes 196616 | tf_op jit(solution)/shard_map/ppermute | solution.py:626
  16.2 4.6 %collective-permute-start.9 = (bf16[2,128,128]{2,1,0:T(8,128)(2,1)S(1)}, bf16[2,128,128]{2,1,0:T(8,128)(2,1)S(1)}, u32[]{:S(2)}, u32[]{:S(2)}) collective-permute-start(bf16[2,128,128]{2,1,0:T(8,128)(2,1)S(1)} %get-tuple-element.59), channel_id=1, source_target_pairs={{0,6},{1,7},{2,4},{3,5},{4,2},{5,3},{6,0},{7,1},{8,14},{9,15},{10,... | collective-permute-start | bytes 196616 | tf_op jit(solution)/shard_map/ppermute | solution.py:626
  18.7 14.9 %collective-permute-start.1 = (bf16[2,256,128]{2,1,0:T(8,128)(2,1)S(1)}, bf16[2,256,128]{2,1,0:T(8,128)(2,1)S(1)}, u32[]{:S(2)}, u32[]{:S(2)}) collective-permute-start(bf16[2,256,128]{2,1,0:T(8,128)(2,1)S(1)} %get-tuple-element.52), channel_id=1, source_target_pairs={{0,2},{1,3},{2,0},{3,1},{4,6},{5,7},{6,4},{7,5},{8,10},{9,11},{10,... | collective-permute-start | bytes 393224 | tf_op jit(solution)/shard_map/ppermute | solution.py:626
  20.8 12.8 %collective-permute-start.2 = (bf16[2,256,128]{2,1,0:T(8,128)(2,1)S(1)}, bf16[2,256,128]{2,1,0:T(8,128)(2,1)S(1)}, u32[]{:S(2)}, u32[]{:S(2)}) collective-permute-start(bf16[2,256,128]{2,1,0:T(8,128)(2,1)S(1)} %get-tuple-element.53), channel_id=1, source_target_pairs={{0,4},{1,5},{2,6},{3,7},{4,0},{5,1},{6,2},{7,3},{8,12},{9,13},{10,... | collective-permute-start | bytes 393224 | tf_op jit(solution)/shard_map/ppermute | solution.py:626
  23.5 10.9 %collective-permute-start.3 = (bf16[2,256,128]{2,1,0:T(8,128)(2,1)S(1)}, bf16[2,256,128]{2,1,0:T(8,128)(2,1)S(1)}, u32[]{:S(2)}, u32[]{:S(2)}) collective-permute-start(bf16[2,256,128]{2,1,0:T(8,128)(2,1)S(1)} %get-tuple-element.54), channel_id=1, source_target_pairs={{0,6},{1,7},{2,4},{3,5},{4,2},{5,3},{6,0},{7,1},{8,14},{9,15},{10,... | collective-permute-start | bytes 393224 | tf_op jit(solution)/shard_map/ppermute | solution.py:626
  25.9 12.3 %collective-permute-start.10 = (bf16[8,128,128]{2,1,0:T(8,128)(2,1)S(1)}, bf16[8,128,128]{2,1,0:T(8,128)(2,1)S(1)}, u32[]{:S(2)}, u32[]{:S(2)}) collective-permute-start(bf16[8,128,128]{2,1,0:T(8,128)(2,1)S(1)} %constant_dynamic-update-slice_fusion.refs_0_), channel_id=1, source_target_pairs={{0,8},{8,0},{16,24},{24,16},{1,9},{9,1},{17,25},{25,17},{2,10},{10... | collective-permute-start | bytes 786440 | tf_op jit(solution)/shard_map/ppermute | solution.py:626
  27.4 7.0 %collective-permute-start.11 = (bf16[8,128,128]{2,1,0:T(8,128)(2,1)S(1)}, bf16[8,128,128]{2,1,0:T(8,128)(2,1)S(1)}, u32[]{:S(2)}, u32[]{:S(2)}) collective-permute-start(bf16[8,128,128]{2,1,0:T(8,128)(2,1)S(1)} %constant_dynamic-update-slice_fusion.refs_0_), channel_id=1, source_target_pairs={{0,16},{8,24},{16,0},{24,8},{1,17},{9,25},{17,1},{25,9},{2,18},{10... | collective-permute-start | bytes 786440 | tf_op jit(solution)/shard_map/ppermute | solution.py:626
  28.9 0.9 %copy-start.1 = (bf16[912,128]{1,0:T(8,128)(2,1)S(1)}, bf16[912,128]{1,0:T(8,128)(2,1)}, u32[]{:S(2)}) copy-start(bf16[912,128]{1,0:T(8,128)(2,1)} %get-tuple-element.60.refs_0_) | copy-start | bytes 700420
  34.4 6.4 %collective-permute-start.12 = (bf16[4,128,128]{2,1,0:T(8,128)(2,1)S(1)}, bf16[4,128,128]{2,1,0:T(8,128)(2,1)S(1)}, u32[]{:S(2)}, u32[]{:S(2)}) collective-permute-start(bf16[4,128,128]{2,1,0:T(8,128)(2,1)S(1)} %slice.56), channel_id=1, source_target_pairs={{0,8},{8,0},{16,24},{24,16},{1,9},{9,1},{17,25},{25,17},{2,10},{10... | collective-permute-start | bytes 393224 | tf_op jit(solution)/shard_map/ppermute | solution.py:626
  36.0 16.7 %collective-permute-start.16 = (bf16[8,128,128]{2,1,0:T(8,128)(2,1)S(1)}, bf16[8,128,128]{2,1,0:T(8,128)(2,1)S(1)}, u32[]{:S(2)}, u32[]{:S(2)}) collective-permute-start(bf16[8,128,128]{2,1,0:T(8,128)(2,1)S(1)} %pad_maximum_fusion.1.refs_0_), channel_id=1, source_target_pairs={{0,8},{8,0},{16,24},{24,16},{1,9},{9,1},{17,25},{25,17},{2,10},{10... | collective-permute-start | bytes 786440 | tf_op jit(solution)/shard_map/ppermute | solution.py:626
  36.6 16.1 %collective-permute-start.17 = (bf16[8,128,128]{2,1,0:T(8,128)(2,1)S(1)}, bf16[8,128,128]{2,1,0:T(8,128)(2,1)S(1)}, u32[]{:S(2)}, u32[]{:S(2)}) collective-permute-start(bf16[8,128,128]{2,1,0:T(8,128)(2,1)S(1)} %pad_maximum_fusion.1.refs_0_), channel_id=1, source_target_pairs={{0,16},{8,24},{16,0},{24,8},{1,17},{9,25},{17,1},{25,9},{2,18},{10... | collective-permute-start | bytes 786440 | tf_op jit(solution)/shard_map/ppermute | solution.py:626
  38.2 10.4 %collective-permute-start.13 = (bf16[4,128,128]{2,1,0:T(8,128)(2,1)S(1)}, bf16[4,128,128]{2,1,0:T(8,128)(2,1)S(1)}, u32[]{:S(2)}, u32[]{:S(2)}) collective-permute-start(bf16[4,128,128]{2,1,0:T(8,128)(2,1)S(1)} %slice.57), channel_id=1, source_target_pairs={{0,16},{8,24},{16,0},{24,8},{1,17},{9,25},{17,1},{25,9},{2,18},{10... | collective-permute-start | bytes 393224 | tf_op jit(solution)/shard_map/ppermute | solution.py:626
  38.8 18.6 %collective-permute-start.14 = (bf16[8,128,128]{2,1,0:T(8,128)(2,1)S(1)}, bf16[8,128,128]{2,1,0:T(8,128)(2,1)S(1)}, u32[]{:S(2)}, u32[]{:S(2)}) collective-permute-start(bf16[8,128,128]{2,1,0:T(8,128)(2,1)S(1)} %pad_maximum_fusion.refs_0_), channel_id=1, source_target_pairs={{0,8},{8,0},{16,24},{24,16},{1,9},{9,1},{17,25},{25,17},{2,10},{10... | collective-permute-start | bytes 786440 | tf_op jit(solution)/shard_map/ppermute | solution.py:626
  40.9 16.5 %collective-permute-start.15 = (bf16[8,128,128]{2,1,0:T(8,128)(2,1)S(1)}, bf16[8,128,128]{2,1,0:T(8,128)(2,1)S(1)}, u32[]{:S(2)}, u32[]{:S(2)}) collective-permute-start(bf16[8,128,128]{2,1,0:T(8,128)(2,1)S(1)} %pad_maximum_fusion.refs_0_), channel_id=1, source_target_pairs={{0,16},{8,24},{16,0},{24,8},{1,17},{9,25},{17,1},{25,9},{2,18},{10... | collective-permute-start | bytes 786440 | tf_op jit(solution)/shard_map/ppermute | solution.py:626
  52.8 7.2 %collective-permute-start.20 = (bf16[4,128,128]{2,1,0:T(8,128)(2,1)S(1)}, bf16[4,128,128]{2,1,0:T(8,128)(2,1)S(1)}, u32[]{:S(2)}, u32[]{:S(2)}) collective-permute-start(bf16[4,128,128]{2,1,0:T(8,128)(2,1)S(1)} %slice.54), channel_id=1, source_target_pairs={{0,8},{8,0},{16,24},{24,16},{1,9},{9,1},{17,25},{25,17},{2,10},{10... | collective-permute-start | bytes 393224 | tf_op jit(solution)/shard_map/ppermute | solution.py:626
  54.4 5.6 %collective-permute-start.21 = (bf16[4,128,128]{2,1,0:T(8,128)(2,1)S(1)}, bf16[4,128,128]{2,1,0:T(8,128)(2,1)S(1)}, u32[]{:S(2)}, u32[]{:S(2)}) collective-permute-start(bf16[4,128,128]{2,1,0:T(8,128)(2,1)S(1)} %slice.55), channel_id=1, source_target_pairs={{0,16},{8,24},{16,0},{24,8},{1,17},{9,25},{17,1},{25,9},{2,18},{10... | collective-permute-start | bytes 393224 | tf_op jit(solution)/shard_map/ppermute | solution.py:626
  57.4 5.3 %collective-permute-start.18 = (bf16[4,128,128]{2,1,0:T(8,128)(2,1)S(1)}, bf16[4,128,128]{2,1,0:T(8,128)(2,1)S(1)}, u32[]{:S(2)}, u32[]{:S(2)}) collective-permute-start(bf16[4,128,128]{2,1,0:T(8,128)(2,1)S(1)} %slice.52), channel_id=1, source_target_pairs={{0,8},{8,0},{16,24},{24,16},{1,9},{9,1},{17,25},{25,17},{2,10},{10... | collective-permute-start | bytes 393224 | tf_op jit(solution)/shard_map/ppermute | solution.py:626
  58.0 5.0 %collective-permute-start.19 = (bf16[4,128,128]{2,1,0:T(8,128)(2,1)S(1)}, bf16[4,128,128]{2,1,0:T(8,128)(2,1)S(1)}, u32[]{:S(2)}, u32[]{:S(2)}) collective-permute-start(bf16[4,128,128]{2,1,0:T(8,128)(2,1)S(1)} %slice.53), channel_id=1, source_target_pairs={{0,16},{8,24},{16,0},{24,8},{1,17},{9,25},{17,1},{25,9},{2,18},{10... | collective-permute-start | bytes 393224 | tf_op jit(solution)/shard_map/ppermute | solution.py:626
